TPU v7x, 512 devices: a whole 4x8x8 slice. The times are simulated.
512 devices in a mesh: tm: 8 (over z), cell: 64 (over x, y, core).
Axes of the slice: x: 4, y: 8, z: 8, core: 2. Of those that a mesh axis runs over, the one named last changes fastest.
Arguments:
- initial: float32 [16384, 128], P('cell'), may hold values from 0.2 to 6, as said below
- source: float32 [16, 16384, 128], P('tm', 'cell'), may hold values from -1.8 to 1.8
- mix_rate: float32 [128], replicated, may hold values from 0.05 to 0.4
- fine_inverse: float32 [16, 128, 128, 128], P('tm', 'cell'), may hold values from -0.1 to 0.9, as said below
- coarse_inverse: float32 [16, 128, 128, 128], P('tm', 'cell'), may hold values from -0.1 to 1, as said below
- step_counts: int32 [16384], P('cell'), may hold values from 4 to 8
Outputs:
- finals: float32 [16, 16384, 128], P('tm', 'cell')
Inputs may be any that keep to these rules, and one draw needn't show every extreme that they name: `initial`: positive compositions. `fine_inverse`: each matrix is a positive diagonal plus small off-diagonal entries. `coarse_inverse`: each matrix is a positive diagonal plus small off-diagonal entries.
All inputs are finite; a program needn't handle non-finite values.
Results may differ from a plain program's by a relative error of at most 0.00011.
Values sent between devices are 32-bit elements; how exact they have to be, the bound alone decides.
A program may use at most 64 MiB of HBM per device.

v0:
```python
import jax
import jax.numpy as jnp
from jax import lax
from jax.sharding import PartitionSpec as P

FINE_MAX = 8
ITERS = 2


def from_behind(block, axis, distance):
    devices = range(lax.axis_size(axis))
    route = [(i - distance, i) for i in devices if i - distance in devices]
    return lax.ppermute(block, axis, route)


def sent_to_all(x, axis):
    count = lax.axis_size(axis)
    return lax.all_to_all(jnp.broadcast_to(x[None], (count, *x.shape)), axis, 0, 0, tiled=True)


def over_copies(x, axis):
    return sent_to_all(x, axis).sum(axis=0)


def group_mul(state, matrices):
    count, width = state.shape
    groups = matrices.shape[0]
    shaped = state.reshape(groups, count // groups, width)
    result = jnp.einsum("gcs,gst->gct", shaped, matrices, precision=lax.Precision.HIGHEST)
    return result.reshape(count, width)


def slices_mul(state, matrices):
    lead, count, width = state.shape
    groups = matrices.shape[1]
    shaped = state.reshape(lead, groups, count // groups, width)
    result = jnp.einsum("lgcs,lgst->lgct", shaped, matrices, precision=lax.Precision.HIGHEST)
    return result.reshape(lead, count, width)


def local_chain(incoming, offsets, coarse_inverse):
    state = incoming
    results = []
    for index in range(offsets.shape[0]):
        state = group_mul(state, coarse_inverse[index]) + offsets[index]
        results.append(state)
    return jnp.stack(results, axis=0)


def zero_start_end(offsets, coarse_inverse):
    state = offsets[0]
    state = group_mul(state, coarse_inverse[1]) + offsets[1]
    return state


def across(initial, offsets, coarse_inverse):
    composed = coarse_inverse[0]
    composed = jnp.einsum(
        "gst,gtu->gsu", composed, coarse_inverse[1], precision=lax.Precision.HIGHEST
    )
    shifted = zero_start_end(offsets, coarse_inverse)
    leading = lax.axis_index("tm") == 0

    def advance(turn, incoming):
        ending = group_mul(incoming, composed) + shifted
        received = from_behind(ending, "tm", 1)
        return jnp.where(leading, initial, received)

    incoming = lax.fori_loop(0, lax.axis_size("tm") - 1, advance, initial)
    return (incoming, local_chain(incoming, offsets, coarse_inverse))


def body(initial, source, mix_rate, fine_inverse, coarse_inverse, step_counts):
    total = initial.shape[0] * lax.axis_size("cell")
    offsets0 = slices_mul(source, coarse_inverse)
    incoming, finals = across(initial, offsets0, coarse_inverse)
    for sweep_round in range(ITERS):
        starts = jnp.concatenate([incoming[None], finals[:-1]], axis=0)
        state = starts
        for substep in range(FINE_MAX):
            average = over_copies(jnp.sum(state, axis=1), "cell") / total
            moved = slices_mul(
                state + source + mix_rate * (average[:, None, :] - state), fine_inverse
            )
            active = (substep < step_counts)[None, :, None]
            state = jnp.where(active, moved, state)
        coarse_ends = slices_mul(starts, coarse_inverse) + offsets0
        offsets = offsets0 + state - coarse_ends
        incoming, finals = across(initial, offsets, coarse_inverse)
    return finals


def solution(mesh):
    return jax.shard_map(
        body,
        mesh=mesh,
        in_specs=(
            P("cell", None),
            P("tm", "cell", None),
            P(),
            P("tm", "cell", None, None),
            P("tm", "cell", None, None),
            P("cell"),
        ),
        out_specs=P("tm", "cell", None),
        check_vma=False,
    )
```

profile of v0, /device:TPU:256, one launch (start us, length us, event | category | flops | bytes accessed | tf_op | source)
XLA Modules:
  0.0 430.7 jit_solution(14056360924680570404)
XLA Ops:
  5.5 59.8 %while.30 = (s32[]{:T(128)}, f32[256,128]{1,0:T(8,128)S(1)}, pred[]{:T(512)}, f32[2,128,128]{2,1,0:T(8,128)S(1)}, f32[256,128]{1,0:T(8,128)S(1)}, /*index=5*/f32[256,128]{1,0:T(8,128)S(1)}, s32[]{:T(128)}) while((s32[]{:T(128)}, f32[256,128]{1,0:T(8,128)S(1)}, pred[]{:T(512)}, f32[2,128,128]{2,1,0:T(8,128)S(1)}, f32[256,128]{1,0:T(8,128)S(1)}, ...), condition=%wide.region_1.2_spmd, body=%wide.region_0.1_spmd.sunk | while | flops 50397184 | bytes 1704054 | solution.py:69
  5.9 3.4 collective-permute-start
  9.2 5.0 %collective-permute-done = f32[256,128]{1,0:T(8,128)S(1)} collective-permute-done((f32[256,128]{1,0:T(8,128)S(1)}, f32[256,128]{1,0:T(8,128)S(1)}, u32[]{:S(2)}, u32[]{:S(2)}) %collective-permute-start) | collective-permute-done | bytes 131104 | tf_op jit(solution)/shard_map/while/body/eval_jaxpr/ppermute | solution.py:13
  14.5 2.2 collective-permute-start
  16.7 5.9 %collective-permute-done = f32[256,128]{1,0:T(8,128)S(1)} collective-permute-done((f32[256,128]{1,0:T(8,128)S(1)}, f32[256,128]{1,0:T(8,128)S(1)}, u32[]{:S(2)}, u32[]{:S(2)}) %collective-permute-start) | collective-permute-done | bytes 131104 | tf_op jit(solution)/shard_map/while/body/eval_jaxpr/ppermute | solution.py:13
  24.9 6.1 %collective-permute-done = f32[256,128]{1,0:T(8,128)S(1)} collective-permute-done((f32[256,128]{1,0:T(8,128)S(1)}, f32[256,128]{1,0:T(8,128)S(1)}, u32[]{:S(2)}, u32[]{:S(2)}) %collective-permute-start) | collective-permute-done | bytes 131104 | tf_op jit(solution)/shard_map/while/body/eval_jaxpr/ppermute | solution.py:13
  33.3 6.1 %collective-permute-done = f32[256,128]{1,0:T(8,128)S(1)} collective-permute-done((f32[256,128]{1,0:T(8,128)S(1)}, f32[256,128]{1,0:T(8,128)S(1)}, u32[]{:S(2)}, u32[]{:S(2)}) %collective-permute-start) | collective-permute-done | bytes 131104 | tf_op jit(solution)/shard_map/while/body/eval_jaxpr/ppermute | solution.py:13
  39.8 1.9 collective-permute-start
  41.7 6.1 %collective-permute-done = f32[256,128]{1,0:T(8,128)S(1)} collective-permute-done((f32[256,128]{1,0:T(8,128)S(1)}, f32[256,128]{1,0:T(8,128)S(1)}, u32[]{:S(2)}, u32[]{:S(2)}) %collective-permute-start) | collective-permute-done | bytes 131104 | tf_op jit(solution)/shard_map/while/body/eval_jaxpr/ppermute | solution.py:13
  50.1 6.9 %collective-permute-done = f32[256,128]{1,0:T(8,128)S(1)} collective-permute-done((f32[256,128]{1,0:T(8,128)S(1)}, f32[256,128]{1,0:T(8,128)S(1)}, u32[]{:S(2)}, u32[]{:S(2)}) %collective-permute-start) | collective-permute-done | bytes 131104 | tf_op jit(solution)/shard_map/while/body/eval_jaxpr/ppermute | solution.py:13
  59.2 6.1 %collective-permute-done = f32[256,128]{1,0:T(8,128)S(1)} collective-permute-done((f32[256,128]{1,0:T(8,128)S(1)}, f32[256,128]{1,0:T(8,128)S(1)}, u32[]{:S(2)}, u32[]{:S(2)}) %collective-permute-start) | collective-permute-done | bytes 131104 | tf_op jit(solution)/shard_map/while/body/eval_jaxpr/ppermute | solution.py:13
  67.1 10.7 %all-to-all-start = ((f32[64,2,128]{2,1,0:T(2,128)}), f32[64,2,128]{2,1,0:T(2,128)S(1)}, u32[]{:S(2)}, u32[]{:S(2)}) async-start(f32[64,2,128]{2,1,0:T(2,128)} %broadcast_in_dim.254), calls=%async_computation | async-start | bytes 131072 | tf_op jit(solution)/shard_map/all_to_all | solution.py:18
  77.8 9.7 %all-to-all-done = f32[64,2,128]{2,1,0:T(2,128)S(1)} async-done(((f32[64,2,128]{2,1,0:T(2,128)}), f32[64,2,128]{2,1,0:T(2,128)S(1)}, u32[]{:S(2)}, u32[]{:S(2)}) %all-to-all-start) | async-done | bytes 65568 | tf_op jit(solution)/shard_map/all_to_all | solution.py:18
  88.8 13.6 %all_to_all.80 = f32[64,2,128]{2,1,0:T(2,128)S(1)} all-to-all(f32[64,2,128]{2,1,0:T(2,128)S(1)} %broadcast_in_dim.257), channel_id=1, replica_groups=mesh['tm'=8,'cell'=64] {'cell'}, dimensions={0} | all-to-all | bytes 131072 | tf_op jit(solution)/shard_map/all_to_all | solution.py:18
  103.0 13.6 %all_to_all.81 = f32[64,2,128]{2,1,0:T(2,128)S(1)} all-to-all(f32[64,2,128]{2,1,0:T(2,128)S(1)} %broadcast_in_dim.260), channel_id=1, replica_groups=mesh['tm'=8,'cell'=64] {'cell'}, dimensions={0} | all-to-all | bytes 131072 | tf_op jit(solution)/shard_map/all_to_all | solution.py:18
  117.3 13.6 %all_to_all.82 = f32[64,2,128]{2,1,0:T(2,128)S(1)} all-to-all(f32[64,2,128]{2,1,0:T(2,128)S(1)} %broadcast_in_dim.263), channel_id=1, replica_groups=mesh['tm'=8,'cell'=64] {'cell'}, dimensions={0} | all-to-all | bytes 131072 | tf_op jit(solution)/shard_map/all_to_all | solution.py:18
  131.7 13.6 %all_to_all.83 = f32[64,2,128]{2,1,0:T(2,128)S(1)} all-to-all(f32[64,2,128]{2,1,0:T(2,128)S(1)} %broadcast_in_dim.266), channel_id=1, replica_groups=mesh['tm'=8,'cell'=64] {'cell'}, dimensions={0} | all-to-all | bytes 131072 | tf_op jit(solution)/shard_map/all_to_all | solution.py:18
  146.0 13.6 %all_to_all.84 = f32[64,2,128]{2,1,0:T(2,128)S(1)} all-to-all(f32[64,2,128]{2,1,0:T(2,128)S(1)} %broadcast_in_dim.269), channel_id=1, replica_groups=mesh['tm'=8,'cell'=64] {'cell'}, dimensions={0} | all-to-all | bytes 131072 | tf_op jit(solution)/shard_map/all_to_all | solution.py:18
  160.9 4.8 %all-to-all-start.6 = ((f32[64,2,128]{2,1,0:T(2,128)}), f32[64,2,128]{2,1,0:T(2,128)S(1)}, u32[]{:S(2)}, u32[]{:S(2)}) async-start(f32[64,2,128]{2,1,0:T(2,128)} %broadcast_in_dim.272), calls=%async_computation.6 | async-start | bytes 131072 | tf_op jit(solution)/shard_map/all_to_all | solution.py:18
  165.7 9.5 %all-to-all-done.6 = f32[64,2,128]{2,1,0:T(2,128)S(1)} async-done(((f32[64,2,128]{2,1,0:T(2,128)}), f32[64,2,128]{2,1,0:T(2,128)S(1)}, u32[]{:S(2)}, u32[]{:S(2)}) %all-to-all-start.6) | async-done | bytes 65568 | tf_op jit(solution)/shard_map/all_to_all | solution.py:18
  176.5 4.6 %all-to-all-start.7 = ((f32[64,2,128]{2,1,0:T(2,128)}), f32[64,2,128]{2,1,0:T(2,128)S(1)}, u32[]{:S(2)}, u32[]{:S(2)}) async-start(f32[64,2,128]{2,1,0:T(2,128)} %broadcast_in_dim.275), calls=%async_computation.7 | async-start | bytes 131072 | tf_op jit(solution)/shard_map/all_to_all | solution.py:18
  181.6 9.3 %all-to-all-done.7 = f32[64,2,128]{2,1,0:T(2,128)S(1)} async-done(((f32[64,2,128]{2,1,0:T(2,128)}), f32[64,2,128]{2,1,0:T(2,128)S(1)}, u32[]{:S(2)}, u32[]{:S(2)}) %all-to-all-start.7) | async-done | bytes 65568 | tf_op jit(solution)/shard_map/all_to_all | solution.py:18
  192.0 59.8 %while.31 = (s32[]{:T(128)}, f32[256,128]{1,0:T(8,128)S(1)}, pred[]{:T(512)}, f32[2,128,128]{2,1,0:T(8,128)S(1)}, f32[256,128]{1,0:T(8,128)S(1)}, /*index=5*/f32[256,128]{1,0:T(8,128)S(1)}, s32[]{:T(128)}) while((s32[]{:T(128)}, f32[256,128]{1,0:T(8,128)S(1)}, pred[]{:T(512)}, f32[2,128,128]{2,1,0:T(8,128)S(1)}, f32[256,128]{1,0:T(8,128)S(1)}, ...), condition=%wide.region_19.20_spmd, body=%wide.region_18.19_spmd.sunk | while | flops 50397184 | bytes 1704054 | solution.py:69
  194.2 6.7 %collective-permute-done.1 = f32[256,128]{1,0:T(8,128)S(1)} collective-permute-done((f32[256,128]{1,0:T(8,128)S(1)}, f32[256,128]{1,0:T(8,128)S(1)}, u32[]{:S(2)}, u32[]{:S(2)}) %collective-permute-start.1) | collective-permute-done | bytes 131104 | tf_op jit(solution)/shard_map/while/body/eval_jaxpr/ppermute | solution.py:13
  203.1 6.1 %collective-permute-done.1 = f32[256,128]{1,0:T(8,128)S(1)} collective-permute-done((f32[256,128]{1,0:T(8,128)S(1)}, f32[256,128]{1,0:T(8,128)S(1)}, u32[]{:S(2)}, u32[]{:S(2)}) %collective-permute-start.1) | collective-permute-done | bytes 131104 | tf_op jit(solution)/shard_map/while/body/eval_jaxpr/ppermute | solution.py:13
  211.6 6.1 %collective-permute-done.1 = f32[256,128]{1,0:T(8,128)S(1)} collective-permute-done((f32[256,128]{1,0:T(8,128)S(1)}, f32[256,128]{1,0:T(8,128)S(1)}, u32[]{:S(2)}, u32[]{:S(2)}) %collective-permute-start.1) | collective-permute-done | bytes 131104 | tf_op jit(solution)/shard_map/while/body/eval_jaxpr/ppermute | solution.py:13
  220.0 6.1 %collective-permute-done.1 = f32[256,128]{1,0:T(8,128)S(1)} collective-permute-done((f32[256,128]{1,0:T(8,128)S(1)}, f32[256,128]{1,0:T(8,128)S(1)}, u32[]{:S(2)}, u32[]{:S(2)}) %collective-permute-start.1) | collective-permute-done | bytes 131104 | tf_op jit(solution)/shard_map/while/body/eval_jaxpr/ppermute | solution.py:13
  228.4 6.1 %collective-permute-done.1 = f32[256,128]{1,0:T(8,128)S(1)} collective-permute-done((f32[256,128]{1,0:T(8,128)S(1)}, f32[256,128]{1,0:T(8,128)S(1)}, u32[]{:S(2)}, u32[]{:S(2)}) %collective-permute-start.1) | collective-permute-done | bytes 131104 | tf_op jit(solution)/shard_map/while/body/eval_jaxpr/ppermute | solution.py:13
  236.8 6.6 %collective-permute-done.1 = f32[256,128]{1,0:T(8,128)S(1)} collective-permute-done((f32[256,128]{1,0:T(8,128)S(1)}, f32[256,128]{1,0:T(8,128)S(1)}, u32[]{:S(2)}, u32[]{:S(2)}) %collective-permute-start.1) | collective-permute-done | bytes 131104 | tf_op jit(solution)/shard_map/while/body/eval_jaxpr/ppermute | solution.py:13
  245.6 6.1 %collective-permute-done.1 = f32[256,128]{1,0:T(8,128)S(1)} collective-permute-done((f32[256,128]{1,0:T(8,128)S(1)}, f32[256,128]{1,0:T(8,128)S(1)}, u32[]{:S(2)}, u32[]{:S(2)}) %collective-permute-start.1) | collective-permute-done | bytes 131104 | tf_op jit(solution)/shard_map/while/body/eval_jaxpr/ppermute | solution.py:13
  252.2 13.6 %all_to_all.85 = f32[64,2,128]{2,1,0:T(2,128)S(1)} all-to-all(f32[64,2,128]{2,1,0:T(2,128)S(1)} %broadcast_in_dim.277), channel_id=1, replica_groups=mesh['tm'=8,'cell'=64] {'cell'}, dimensions={0} | all-to-all | bytes 131072 | tf_op jit(solution)/shard_map/all_to_all | solution.py:18
  266.4 13.6 %all_to_all.86 = f32[64,2,128]{2,1,0:T(2,128)S(1)} all-to-all(f32[64,2,128]{2,1,0:T(2,128)S(1)} %broadcast_in_dim.278), channel_id=1, replica_groups=mesh['tm'=8,'cell'=64] {'cell'}, dimensions={0} | all-to-all | bytes 131072 | tf_op jit(solution)/shard_map/all_to_all | solution.py:18
  280.7 13.6 %all_to_all.87 = f32[64,2,128]{2,1,0:T(2,128)S(1)} all-to-all(f32[64,2,128]{2,1,0:T(2,128)S(1)} %broadcast_in_dim.279), channel_id=1, replica_groups=mesh['tm'=8,'cell'=64] {'cell'}, dimensions={0} | all-to-all | bytes 131072 | tf_op jit(solution)/shard_map/all_to_all | solution.py:18
  295.0 13.6 %all_to_all.88 = f32[64,2,128]{2,1,0:T(2,128)S(1)} all-to-all(f32[64,2,128]{2,1,0:T(2,128)S(1)} %broadcast_in_dim.280), channel_id=1, replica_groups=mesh['tm'=8,'cell'=64] {'cell'}, dimensions={0} | all-to-all | bytes 131072 | tf_op jit(solution)/shard_map/all_to_all | solution.py:18
  309.3 13.6 %all_to_all.89 = f32[64,2,128]{2,1,0:T(2,128)S(1)} all-to-all(f32[64,2,128]{2,1,0:T(2,128)S(1)} %broadcast_in_dim.281), channel_id=1, replica_groups=mesh['tm'=8,'cell'=64] {'cell'}, dimensions={0} | all-to-all | bytes 131072 | tf_op jit(solution)/shard_map/all_to_all | solution.py:18
  323.6 13.6 %all_to_all.90 = f32[64,2,128]{2,1,0:T(2,128)S(1)} all-to-all(f32[64,2,128]{2,1,0:T(2,128)S(1)} %broadcast_in_dim.282), channel_id=1, replica_groups=mesh['tm'=8,'cell'=64] {'cell'}, dimensions={0} | all-to-all | bytes 131072 | tf_op jit(solution)/shard_map/all_to_all | solution.py:18
  338.5 4.6 %all-to-all-start.14 = ((f32[64,2,128]{2,1,0:T(2,128)}), f32[64,2,128]{2,1,0:T(2,128)S(1)}, u32[]{:S(2)}, u32[]{:S(2)}) async-start(f32[64,2,128]{2,1,0:T(2,128)} %broadcast_in_dim.283), calls=%async_computation.14 | async-start | bytes 131072 | tf_op jit(solution)/shard_map/all_to_all | solution.py:18
  343.2 9.7 %all-to-all-done.14 = f32[64,2,128]{2,1,0:T(2,128)S(1)} async-done(((f32[64,2,128]{2,1,0:T(2,128)}), f32[64,2,128]{2,1,0:T(2,128)S(1)}, u32[]{:S(2)}, u32[]{:S(2)}) %all-to-all-start.14) | async-done | bytes 65568 | tf_op jit(solution)/shard_map/all_to_all | solution.py:18
  354.2 4.6 %all-to-all-start.15 = ((f32[64,2,128]{2,1,0:T(2,128)}), f32[64,2,128]{2,1,0:T(2,128)S(1)}, u32[]{:S(2)}, u32[]{:S(2)}) async-start(f32[64,2,128]{2,1,0:T(2,128)} %broadcast_in_dim.284), calls=%async_computation.15 | async-start | bytes 131072 | tf_op jit(solution)/shard_map/all_to_all | solution.py:18
  359.2 9.3 %all-to-all-done.15 = f32[64,2,128]{2,1,0:T(2,128)S(1)} async-done(((f32[64,2,128]{2,1,0:T(2,128)}), f32[64,2,128]{2,1,0:T(2,128)S(1)}, u32[]{:S(2)}, u32[]{:S(2)}) %all-to-all-start.15) | async-done | bytes 65568 | tf_op jit(solution)/shard_map/all_to_all | solution.py:18
  369.6 59.8 %while.32 = (s32[]{:T(128)}, f32[256,128]{1,0:T(8,128)S(1)}, pred[]{:T(512)}, f32[2,128,128]{2,1,0:T(8,128)S(1)}, f32[256,128]{1,0:T(8,128)S(1)}, /*index=5*/f32[256,128]{1,0:T(8,128)S(1)}, s32[]{:T(128)}) while((s32[]{:T(128)}, f32[256,128]{1,0:T(8,128)S(1)}, pred[]{:T(512)}, f32[2,128,128]{2,1,0:T(8,128)S(1)}, f32[256,128]{1,0:T(8,128)S(1)}, ...), condition=%wide.region_37.38_spmd, body=%wide.region_36.37_spmd.sunk | while | flops 50397184 | bytes 1704054 | solution.py:69
  371.8 6.7 %collective-permute-done.2 = f32[256,128]{1,0:T(8,128)S(1)} collective-permute-done((f32[256,128]{1,0:T(8,128)S(1)}, f32[256,128]{1,0:T(8,128)S(1)}, u32[]{:S(2)}, u32[]{:S(2)}) %collective-permute-start.2) | collective-permute-done | bytes 131104 | tf_op jit(solution)/shard_map/while/body/eval_jaxpr/ppermute | solution.py:13
  380.8 6.1 %collective-permute-done.2 = f32[256,128]{1,0:T(8,128)S(1)} collective-permute-done((f32[256,128]{1,0:T(8,128)S(1)}, f32[256,128]{1,0:T(8,128)S(1)}, u32[]{:S(2)}, u32[]{:S(2)}) %collective-permute-start.2) | collective-permute-done | bytes 131104 | tf_op jit(solution)/shard_map/while/body/eval_jaxpr/ppermute | solution.py:13
  389.2 6.1 %collective-permute-done.2 = f32[256,128]{1,0:T(8,128)S(1)} collective-permute-done((f32[256,128]{1,0:T(8,128)S(1)}, f32[256,128]{1,0:T(8,128)S(1)}, u32[]{:S(2)}, u32[]{:S(2)}) %collective-permute-start.2) | collective-permute-done | bytes 131104 | tf_op jit(solution)/shard_map/while/body/eval_jaxpr/ppermute | solution.py:13
  397.6 6.1 %collective-permute-done.2 = f32[256,128]{1,0:T(8,128)S(1)} collective-permute-done((f32[256,128]{1,0:T(8,128)S(1)}, f32[256,128]{1,0:T(8,128)S(1)}, u32[]{:S(2)}, u32[]{:S(2)}) %collective-permute-start.2) | collective-permute-done | bytes 131104 | tf_op jit(solution)/shard_map/while/body/eval_jaxpr/ppermute | solution.py:13
  406.0 6.1 %collective-permute-done.2 = f32[256,128]{1,0:T(8,128)S(1)} collective-permute-done((f32[256,128]{1,0:T(8,128)S(1)}, f32[256,128]{1,0:T(8,128)S(1)}, u32[]{:S(2)}, u32[]{:S(2)}) %collective-permute-start.2) | collective-permute-done | bytes 131104 | tf_op jit(solution)/shard_map/while/body/eval_jaxpr/ppermute | solution.py:13
  414.4 6.6 %collective-permute-done.2 = f32[256,128]{1,0:T(8,128)S(1)} collective-permute-done((f32[256,128]{1,0:T(8,128)S(1)}, f32[256,128]{1,0:T(8,128)S(1)}, u32[]{:S(2)}, u32[]{:S(2)}) %collective-permute-start.2) | collective-permute-done | bytes 131104 | tf_op jit(solution)/shard_map/while/body/eval_jaxpr/ppermute | solution.py:13
  423.3 6.1 %collective-permute-done.2 = f32[256,128]{1,0:T(8,128)S(1)} collective-permute-done((f32[256,128]{1,0:T(8,128)S(1)}, f32[256,128]{1,0:T(8,128)S(1)}, u32[]{:S(2)}, u32[]{:S(2)}) %collective-permute-start.2) | collective-permute-done | bytes 131104 | tf_op jit(solution)/shard_map/while/body/eval_jaxpr/ppermute | solution.py:13
  (210 shorter events, 64.8 us)
Async XLA Ops:
  0.0 88.3 %copy-start = (f32[2,2,128,128]{3,2,1,0:T(8,128)S(1)}, f32[2,2,128,128]{3,2,1,0:T(8,128)}, u32[]{:S(2)}) copy-start(f32[2,2,128,128]{3,2,1,0:T(8,128)} %param.15) | copy-start | bytes 786436
  0.0 1.3 copy-start.1
  2.7 1.3 copy-start.4
  2.7 1.0 copy-start.3
  3.7 0.9 copy-start.2
  4.6 0.9 slice-start
  5.9 8.3 %collective-permute-start = (f32[256,128]{1,0:T(8,128)S(1)}, f32[256,128]{1,0:T(8,128)S(1)}, u32[]{:S(2)}, u32[]{:S(2)}) collective-permute-start(f32[256,128]{1,0:T(8,128)S(1)} %bitcast_add_fusion.15), channel_id=1, source_target_pairs={{0,64},{64,128},{128,192},{192,256},{256,320},{320,384},{384,448},... | collective-permute-start | bytes 393224 | tf_op jit(solution)/shard_map/while/body/eval_jaxpr/ppermute | solution.py:13
  14.5 8.1 %collective-permute-start = (f32[256,128]{1,0:T(8,128)S(1)}, f32[256,128]{1,0:T(8,128)S(1)}, u32[]{:S(2)}, u32[]{:S(2)}) collective-permute-start(f32[256,128]{1,0:T(8,128)S(1)} %bitcast_add_fusion.15), channel_id=1, source_target_pairs={{0,64},{64,128},{128,192},{192,256},{256,320},{320,384},{384,448},... | collective-permute-start | bytes 393224 | tf_op jit(solution)/shard_map/while/body/eval_jaxpr/ppermute | solution.py:13
  22.9 8.1 %collective-permute-start = (f32[256,128]{1,0:T(8,128)S(1)}, f32[256,128]{1,0:T(8,128)S(1)}, u32[]{:S(2)}, u32[]{:S(2)}) collective-permute-start(f32[256,128]{1,0:T(8,128)S(1)} %bitcast_add_fusion.15), channel_id=1, source_target_pairs={{0,64},{64,128},{128,192},{192,256},{256,320},{320,384},{384,448},... | collective-permute-start | bytes 393224 | tf_op jit(solution)/shard_map/while/body/eval_jaxpr/ppermute | solution.py:13
  31.3 8.1 %collective-permute-start = (f32[256,128]{1,0:T(8,128)S(1)}, f32[256,128]{1,0:T(8,128)S(1)}, u32[]{:S(2)}, u32[]{:S(2)}) collective-permute-start(f32[256,128]{1,0:T(8,128)S(1)} %bitcast_add_fusion.15), channel_id=1, source_target_pairs={{0,64},{64,128},{128,192},{192,256},{256,320},{320,384},{384,448},... | collective-permute-start | bytes 393224 | tf_op jit(solution)/shard_map/while/body/eval_jaxpr/ppermute | solution.py:13
  39.8 8.1 %collective-permute-start = (f32[256,128]{1,0:T(8,128)S(1)}, f32[256,128]{1,0:T(8,128)S(1)}, u32[]{:S(2)}, u32[]{:S(2)}) collective-permute-start(f32[256,128]{1,0:T(8,128)S(1)} %bitcast_add_fusion.15), channel_id=1, source_target_pairs={{0,64},{64,128},{128,192},{192,256},{256,320},{320,384},{384,448},... | collective-permute-start | bytes 393224 | tf_op jit(solution)/shard_map/while/body/eval_jaxpr/ppermute | solution.py:13
  48.2 8.8 %collective-permute-start = (f32[256,128]{1,0:T(8,128)S(1)}, f32[256,128]{1,0:T(8,128)S(1)}, u32[]{:S(2)}, u32[]{:S(2)}) collective-permute-start(f32[256,128]{1,0:T(8,128)S(1)} %bitcast_add_fusion.15), channel_id=1, source_target_pairs={{0,64},{64,128},{128,192},{192,256},{256,320},{320,384},{384,448},... | collective-permute-start | bytes 393224 | tf_op jit(solution)/shard_map/while/body/eval_jaxpr/ppermute | solution.py:13
  57.3 8.1 %collective-permute-start = (f32[256,128]{1,0:T(8,128)S(1)}, f32[256,128]{1,0:T(8,128)S(1)}, u32[]{:S(2)}, u32[]{:S(2)}) collective-permute-start(f32[256,128]{1,0:T(8,128)S(1)} %bitcast_add_fusion.15), channel_id=1, source_target_pairs={{0,64},{64,128},{128,192},{192,256},{256,320},{320,384},{384,448},... | collective-permute-start | bytes 393224 | tf_op jit(solution)/shard_map/while/body/eval_jaxpr/ppermute | solution.py:13
  65.4 1.0 copy-start.5
  67.1 10.7 %copy-start.7 = (s32[256]{0:T(256)S(1)}, s32[256]{0:T(256)}, u32[]{:S(2)}) copy-start(s32[256]{0:T(256)} %param.17) | copy-start | bytes 3076
  67.1 20.4 %all-to-all-start = ((f32[64,2,128]{2,1,0:T(2,128)}), f32[64,2,128]{2,1,0:T(2,128)S(1)}, u32[]{:S(2)}, u32[]{:S(2)}) async-start(f32[64,2,128]{2,1,0:T(2,128)} %broadcast_in_dim.254), calls=%async_computation | async-start | bytes 131072 | tf_op jit(solution)/shard_map/all_to_all | solution.py:18
  87.6 0.7 copy-start.6
  160.9 14.3 %all-to-all-start.6 = ((f32[64,2,128]{2,1,0:T(2,128)}), f32[64,2,128]{2,1,0:T(2,128)S(1)}, u32[]{:S(2)}, u32[]{:S(2)}) async-start(f32[64,2,128]{2,1,0:T(2,128)} %broadcast_in_dim.272), calls=%async_computation.6 | async-start | bytes 131072 | tf_op jit(solution)/shard_map/all_to_all | solution.py:18
  176.5 14.3 %all-to-all-start.7 = ((f32[64,2,128]{2,1,0:T(2,128)}), f32[64,2,128]{2,1,0:T(2,128)S(1)}, u32[]{:S(2)}, u32[]{:S(2)}) async-start(f32[64,2,128]{2,1,0:T(2,128)} %broadcast_in_dim.275), calls=%async_computation.7 | async-start | bytes 131072 | tf_op jit(solution)/shard_map/all_to_all | solution.py:18
  192.3 8.6 %collective-permute-start.1 = (f32[256,128]{1,0:T(8,128)S(1)}, f32[256,128]{1,0:T(8,128)S(1)}, u32[]{:S(2)}, u32[]{:S(2)}) collective-permute-start(f32[256,128]{1,0:T(8,128)S(1)} %bitcast_add_fusion.16), channel_id=1, source_target_pairs={{0,64},{64,128},{128,192},{192,256},{256,320},{320,384},{384,448},... | collective-permute-start | bytes 393224 | tf_op jit(solution)/shard_map/while/body/eval_jaxpr/ppermute | solution.py:13
  201.2 8.1 %collective-permute-start.1 = (f32[256,128]{1,0:T(8,128)S(1)}, f32[256,128]{1,0:T(8,128)S(1)}, u32[]{:S(2)}, u32[]{:S(2)}) collective-permute-start(f32[256,128]{1,0:T(8,128)S(1)} %bitcast_add_fusion.16), channel_id=1, source_target_pairs={{0,64},{64,128},{128,192},{192,256},{256,320},{320,384},{384,448},... | collective-permute-start | bytes 393224 | tf_op jit(solution)/shard_map/while/body/eval_jaxpr/ppermute | solution.py:13
  209.6 8.1 %collective-permute-start.1 = (f32[256,128]{1,0:T(8,128)S(1)}, f32[256,128]{1,0:T(8,128)S(1)}, u32[]{:S(2)}, u32[]{:S(2)}) collective-permute-start(f32[256,128]{1,0:T(8,128)S(1)} %bitcast_add_fusion.16), channel_id=1, source_target_pairs={{0,64},{64,128},{128,192},{192,256},{256,320},{320,384},{384,448},... | collective-permute-start | bytes 393224 | tf_op jit(solution)/shard_map/while/body/eval_jaxpr/ppermute | solution.py:13
  218.0 8.1 %collective-permute-start.1 = (f32[256,128]{1,0:T(8,128)S(1)}, f32[256,128]{1,0:T(8,128)S(1)}, u32[]{:S(2)}, u32[]{:S(2)}) collective-permute-start(f32[256,128]{1,0:T(8,128)S(1)} %bitcast_add_fusion.16), channel_id=1, source_target_pairs={{0,64},{64,128},{128,192},{192,256},{256,320},{320,384},{384,448},... | collective-permute-start | bytes 393224 | tf_op jit(solution)/shard_map/while/body/eval_jaxpr/ppermute | solution.py:13
  226.4 8.1 %collective-permute-start.1 = (f32[256,128]{1,0:T(8,128)S(1)}, f32[256,128]{1,0:T(8,128)S(1)}, u32[]{:S(2)}, u32[]{:S(2)}) collective-permute-start(f32[256,128]{1,0:T(8,128)S(1)} %bitcast_add_fusion.16), channel_id=1, source_target_pairs={{0,64},{64,128},{128,192},{192,256},{256,320},{320,384},{384,448},... | collective-permute-start | bytes 393224 | tf_op jit(solution)/shard_map/while/body/eval_jaxpr/ppermute | solution.py:13
  234.8 8.5 %collective-permute-start.1 = (f32[256,128]{1,0:T(8,128)S(1)}, f32[256,128]{1,0:T(8,128)S(1)}, u32[]{:S(2)}, u32[]{:S(2)}) collective-permute-start(f32[256,128]{1,0:T(8,128)S(1)} %bitcast_add_fusion.16), channel_id=1, source_target_pairs={{0,64},{64,128},{128,192},{192,256},{256,320},{320,384},{384,448},... | collective-permute-start | bytes 393224 | tf_op jit(solution)/shard_map/while/body/eval_jaxpr/ppermute | solution.py:13
  243.7 8.1 %collective-permute-start.1 = (f32[256,128]{1,0:T(8,128)S(1)}, f32[256,128]{1,0:T(8,128)S(1)}, u32[]{:S(2)}, u32[]{:S(2)}) collective-permute-start(f32[256,128]{1,0:T(8,128)S(1)} %bitcast_add_fusion.16), channel_id=1, source_target_pairs={{0,64},{64,128},{128,192},{192,256},{256,320},{320,384},{384,448},... | collective-permute-start | bytes 393224 | tf_op jit(solution)/shard_map/while/body/eval_jaxpr/ppermute | solution.py:13
  338.5 14.3 %all-to-all-start.14 = ((f32[64,2,128]{2,1,0:T(2,128)}), f32[64,2,128]{2,1,0:T(2,128)S(1)}, u32[]{:S(2)}, u32[]{:S(2)}) async-start(f32[64,2,128]{2,1,0:T(2,128)} %broadcast_in_dim.283), calls=%async_computation.14 | async-start | bytes 131072 | tf_op jit(solution)/shard_map/all_to_all | solution.py:18
  354.2 14.3 %all-to-all-start.15 = ((f32[64,2,128]{2,1,0:T(2,128)}), f32[64,2,128]{2,1,0:T(2,128)S(1)}, u32[]{:S(2)}, u32[]{:S(2)}) async-start(f32[64,2,128]{2,1,0:T(2,128)} %broadcast_in_dim.284), calls=%async_computation.15 | async-start | bytes 131072 | tf_op jit(solution)/shard_map/all_to_all | solution.py:18
  369.9 8.6 %collective-permute-start.2 = (f32[256,128]{1,0:T(8,128)S(1)}, f32[256,128]{1,0:T(8,128)S(1)}, u32[]{:S(2)}, u32[]{:S(2)}) collective-permute-start(f32[256,128]{1,0:T(8,128)S(1)} %bitcast_add_fusion.17), channel_id=1, source_target_pairs={{0,64},{64,128},{128,192},{192,256},{256,320},{320,384},{384,448},... | collective-permute-start | bytes 393224 | tf_op jit(solution)/shard_map/while/body/eval_jaxpr/ppermute | solution.py:13
  378.8 8.1 %collective-permute-start.2 = (f32[256,128]{1,0:T(8,128)S(1)}, f32[256,128]{1,0:T(8,128)S(1)}, u32[]{:S(2)}, u32[]{:S(2)}) collective-permute-start(f32[256,128]{1,0:T(8,128)S(1)} %bitcast_add_fusion.17), channel_id=1, source_target_pairs={{0,64},{64,128},{128,192},{192,256},{256,320},{320,384},{384,448},... | collective-permute-start | bytes 393224 | tf_op jit(solution)/shard_map/while/body/eval_jaxpr/ppermute | solution.py:13
  387.3 8.1 %collective-permute-start.2 = (f32[256,128]{1,0:T(8,128)S(1)}, f32[256,128]{1,0:T(8,128)S(1)}, u32[]{:S(2)}, u32[]{:S(2)}) collective-permute-start(f32[256,128]{1,0:T(8,128)S(1)} %bitcast_add_fusion.17), channel_id=1, source_target_pairs={{0,64},{64,128},{128,192},{192,256},{256,320},{320,384},{384,448},... | collective-permute-start | bytes 393224 | tf_op jit(solution)/shard_map/while/body/eval_jaxpr/ppermute | solution.py:13
  395.7 8.1 %collective-permute-start.2 = (f32[256,128]{1,0:T(8,128)S(1)}, f32[256,128]{1,0:T(8,128)S(1)}, u32[]{:S(2)}, u32[]{:S(2)}) collective-permute-start(f32[256,128]{1,0:T(8,128)S(1)} %bitcast_add_fusion.17), channel_id=1, source_target_pairs={{0,64},{64,128},{128,192},{192,256},{256,320},{320,384},{384,448},... | collective-permute-start | bytes 393224 | tf_op jit(solution)/shard_map/while/body/eval_jaxpr/ppermute | solution.py:13
  404.1 8.1 %collective-permute-start.2 = (f32[256,128]{1,0:T(8,128)S(1)}, f32[256,128]{1,0:T(8,128)S(1)}, u32[]{:S(2)}, u32[]{:S(2)}) collective-permute-start(f32[256,128]{1,0:T(8,128)S(1)} %bitcast_add_fusion.17), channel_id=1, source_target_pairs={{0,64},{64,128},{128,192},{192,256},{256,320},{320,384},{384,448},... | collective-permute-start | bytes 393224 | tf_op jit(solution)/shard_map/while/body/eval_jaxpr/ppermute | solution.py:13
  412.5 8.5 %collective-permute-start.2 = (f32[256,128]{1,0:T(8,128)S(1)}, f32[256,128]{1,0:T(8,128)S(1)}, u32[]{:S(2)}, u32[]{:S(2)}) collective-permute-start(f32[256,128]{1,0:T(8,128)S(1)} %bitcast_add_fusion.17), channel_id=1, source_target_pairs={{0,64},{64,128},{128,192},{192,256},{256,320},{320,384},{384,448},... | collective-permute-start | bytes 393224 | tf_op jit(solution)/shard_map/while/body/eval_jaxpr/ppermute | solution.py:13
  421.3 8.1 %collective-permute-start.2 = (f32[256,128]{1,0:T(8,128)S(1)}, f32[256,128]{1,0:T(8,128)S(1)}, u32[]{:S(2)}, u32[]{:S(2)}) collective-permute-start(f32[256,128]{1,0:T(8,128)S(1)} %bitcast_add_fusion.17), channel_id=1, source_target_pairs={{0,64},{64,128},{128,192},{192,256},{256,320},{320,384},{384,448},... | collective-permute-start | bytes 393224 | tf_op jit(solution)/shard_map/while/body/eval_jaxpr/ppermute | solution.py:13
  430.0 0.7 copy-start.8
where the time goes:
time: 432 us; the launch traced here: 431 us
  waiting for transfers between devices  178 us (41%)
  blocking collectives  150 us (35%)
  starting transfers between devices  71.4 us (17%)
  matrix products  17.7 us (4%)
  local copies, waits for them, and re-layouts  8.13 us (2%)
  other arithmetic  4.37 us (1%)
    all_to_all x11, blocking collectives, sent_to_all(): lax.all_to_all(jnp.broadcast_to(x[None], (count, *x.shape)), axis, 0, 0,...  150 us
    ppermute x21, waiting for transfers between devices, from_behind(): return lax.ppermute(block, axis, route)  130 us
    all_to_all x5, waiting for transfers between devices, sent_to_all(): lax.all_to_all(jnp.broadcast_to(x[None], (count, *x.shape)), axis, 0, 0,...  47.5 us
    ppermute x21, starting transfers between devices, from_behind(): return lax.ppermute(block, axis, route)  42 us
    all_to_all x5, starting transfers between devices, sent_to_all(): lax.all_to_all(jnp.broadcast_to(x[None], (count, *x.shape)), axis, 0, 0,...  29.3 us
    dot_general x19, matrix products, slices_mul(): jnp.einsum('lgcs,lgst->lgct', shaped, matrices, precision=lax.Precision.H...  8.98 us
  transfers between devices with their start and end apart: 26, of which 26 were waited for; matrix products, arithmetic and copies ran while one was open for 0% of the time, Pallas kernels for 0%

commit v1 on v0

v1 whole, which is shorter than its diff:
```python
import jax
import jax.numpy as jnp
from jax import lax
from jax.experimental import pallas as pl
from jax.experimental.pallas import tpu as pltpu
from jax.sharding import PartitionSpec as P

FINE_MAX = 8
ITERS = 2
FEWEST = 4
CLASSES = 5
MESH = pl.DeviceIdType.MESH
F32 = jnp.float32
BF16 = jnp.bfloat16
XS, YS, CORES = 4, 8, 2
NCHUNK = 8


def split(a):
    high = a.astype(BF16)
    low = (a - high.astype(F32)).astype(BF16)
    return jnp.concatenate([high, low], axis=1)


def put_weights(ref, matrix):
    width = matrix.shape[0]
    pair = split(matrix)
    ref[0:width, :] = pair
    ref[width : 2 * width, :] = pair


def halves(a):
    width = a.shape[1] // 2
    return a[:, :width] + a[:, width:]


def mul(a, weights):
    return halves(jnp.dot(split(a), weights[...], preferred_element_type=F32))


def class_sums(onehot, cells):
    return halves(jnp.dot(onehot, split(cells), preferred_element_type=F32))


def pick(rows, counts):
    out = jnp.broadcast_to(rows[0:1], counts.shape)
    for j in range(1, CLASSES):
        out = jnp.where(counts == float(FEWEST + j), rows[j : j + 1], out)
    return out


def cell_peers():
    me = lax.axis_index("cell")
    core, y, x = me % CORES, (me // CORES) % YS, me // (CORES * YS)
    steps = [
        (min(dx, XS - dx) + min(dy, YS - dy), dx, dy, dc)
        for dx in range(XS)
        for dy in range(YS)
        for dc in range(CORES)
        if dx or dy or dc
    ]
    steps.sort(reverse=True)
    return [
        (((x + dx) % XS) * YS + (y + dy) % YS) * CORES + (core + dc) % CORES
        for _, dx, dy, dc in steps
    ]


def kernel(
    initial, source, mix, fine, coarse, steps, out,
    wf, wc, wp, state, starts, off, shifted, counts, sums, weights_n,
    sbuf, rbuf, zs, zr, ssem, rsem, zssem, zrsem,
):
    lead, count, width = source.shape
    groups = fine.shape[1]
    per = count // groups
    tm = lax.axis_index("tm")
    last = lax.axis_size("tm") - 1
    peers = cell_peers()
    cells = count * lax.axis_size("cell")
    chunk = count // NCHUNK

    barrier = pltpu.get_barrier_semaphore()
    for peer in peers:
        pl.semaphore_signal(barrier, inc=1, device_id={"cell": peer}, device_id_type=MESH)
    behind = lax.rem(tm + last, last + 1)
    pl.semaphore_signal(barrier, inc=1, device_id={"tm": behind}, device_id_type=MESH)

    def rows(g):
        return pl.ds(g * per, per)

    rate = mix[...]
    keep = 1.0 - rate
    row_ids = lax.broadcasted_iota(jnp.int32, (8, width), 0)
    limits = jnp.concatenate([jnp.where(row_ids < CLASSES, row_ids + FEWEST, 0)] * 2, axis=0)
    onehots = []
    for g in range(groups):
        for l in range(lead):
            put_weights(wf.at[l, g], fine[l, g])
            put_weights(wc.at[l, g], coarse[l, g])
        put_weights(wp.at[g], mul(coarse[0, g], wc.at[1, g]))
        line = steps[g : g + 1, :]
        hot = jnp.where(line == row_ids + FEWEST, 1.0, 0.0).astype(F32)
        onehots.append(hot.astype(BF16))
        number = jnp.sum(hot, axis=1, keepdims=True)
        ones = jnp.where(row_ids < CLASSES, 1.0, 0.0).astype(F32)
        weights_n[g] = jnp.concatenate([number * rate, ones * rate], axis=0)
        counts[g] = jnp.broadcast_to(line.astype(F32), (per, width)).T
        for l in range(lead):
            cells_l = source[l, rows(g)]
            summed = class_sums(onehots[g], cells_l)
            sums[l, g] = jnp.concatenate([summed, jnp.zeros_like(summed)], axis=0)
            off[l, rows(g)] = mul(cells_l, wc.at[l, g])
        shifted[rows(g)] = mul(off[0, rows(g)], wc.at[1, g]) + off[1, rows(g)]

    @pl.when(tm == 0)
    def _():
        for k in range(ITERS + 1):
            zr[k] = initial[...]

    pl.semaphore_wait(barrier, len(peers) + 1)

    def hop(k, j):
        part = pl.ds(j * chunk, chunk)
        return pltpu.make_async_remote_copy(
            src_ref=zs.at[k, part],
            dst_ref=zr.at[k, part],
            send_sem=zssem.at[k * NCHUNK + j],
            recv_sem=zrsem.at[k * NCHUNK + j],
            device_id={"tm": lax.rem(tm + 1, last + 1)},
            device_id_type=MESH,
        )

    def chain(k):
        for j in range(NCHUNK):
            part = pl.ds(j * chunk, chunk)

            @pl.when(tm > 0)
            def _():
                hop(k, j).wait_recv()

            ending = mul(zr[k, part], wp.at[j * chunk // per]) + shifted[part]
            zs[k, part] = ending

            @pl.when(tm < last)
            def _():
                hop(k, j).start()

    chain(0)

    def sweep(it, carry):
        y = {}
        for g in range(groups):
            first = zr[it, rows(g)]
            second = mul(first, wc.at[0, g]) + off[0, rows(g)]
            starts[1, rows(g)] = second
            for l, begin in ((0, first), (1, second)):
                state[l, rows(g)] = begin
                summed = class_sums(onehots[g], begin)
                y[l, g] = jnp.concatenate([summed, jnp.zeros_like(summed)], axis=0)

        def fine_cells(m):
            for l in range(lead):
                for g in range(groups):
                    old = state[l, rows(g)]
                    new = mul(old * keep + source[l, rows(g)], wf.at[l, g])
                    if m >= FEWEST:
                        new = jnp.where(counts[g] > float(m), new, old)
                    state[l, rows(g)] = new

        for m in range(FINE_MAX):
            turn = it * FINE_MAX + m
            own = jnp.concatenate(
                [
                    jnp.sum(sum(y[l, g][0:8] for g in range(groups)), axis=0, keepdims=True)
                    for l in range(lead)
                ],
                axis=0,
            )
            sbuf[turn] = own
            for slot, peer in enumerate(peers):
                pltpu.make_async_remote_copy(
                    src_ref=sbuf.at[turn],
                    dst_ref=rbuf.at[turn, slot],
                    send_sem=ssem.at[turn],
                    recv_sem=rsem.at[turn],
                    device_id={"cell": peer},
                    device_id_type=MESH,
                ).start()
            if m < FINE_MAX // 2:
                fine_cells(2 * m)
                fine_cells(2 * m + 1)
            elif m == FINE_MAX // 2:
                for g in range(groups):
                    for l in range(lead):
                        begin = zr[it, rows(g)] if l == 0 else starts[1, rows(g)]
                        off[l, rows(g)] = state[l, rows(g)] - mul(begin, wc.at[l, g])
                    shifted[rows(g)] = mul(off[0, rows(g)], wc.at[1, g]) + off[1, rows(g)]
            pltpu.make_async_copy(rbuf.at[turn], rbuf.at[turn], rsem.at[turn]).wait()
            average = (own + jnp.sum(rbuf[turn], axis=0)) * (1.0 / cells)
            for l in range(lead):
                for g in range(groups):
                    old = y[l, g]
                    fed = old * keep + weights_n[g] * average[l : l + 1] + sums[l, g]
                    new = mul(fed, wf.at[l, g])
                    y[l, g] = jnp.where(limits > m, new, old) if m >= FEWEST else new
        for g in range(groups):
            extra = mul(y[0, g], wc.at[1, g]) + y[1, g]
            shifted[rows(g)] += pick(extra[8:16], counts[g])
        chain(it + 1)
        for g in range(groups):
            off[0, rows(g)] += pick(y[0, g][8:16], counts[g])
        return carry

    lax.fori_loop(0, ITERS, sweep, 0)

    for g in range(groups):
        out[0, rows(g)] = mul(zr[ITERS, rows(g)], wc.at[0, g]) + off[0, rows(g)]
        out[1, rows(g)] = zs[ITERS, rows(g)]

    def drain(turn, carry):
        pltpu.make_async_copy(rbuf.at[turn], rbuf.at[turn], ssem.at[turn]).wait()
        return carry

    lax.fori_loop(0, ITERS * FINE_MAX, drain, 0)

    @pl.when(tm < last)
    def _():
        for k in range(ITERS + 1):
            for j in range(NCHUNK):
                hop(k, j).wait_send()


def body(initial, source, mix_rate, fine_inverse, coarse_inverse, step_counts):
    lead, count, width = source.shape
    groups = fine_inverse.shape[1]
    turns = ITERS * FINE_MAX
    peers = XS * YS * CORES - 1
    vmem = pl.BlockSpec(memory_space=pltpu.VMEM)
    return pl.pallas_call(
        kernel,
        out_shape=jax.ShapeDtypeStruct(source.shape, F32),
        in_specs=[vmem] * 6,
        out_specs=vmem,
        scratch_shapes=[
            pltpu.VMEM((lead, groups, 2 * width, 2 * width), BF16),
            pltpu.VMEM((lead, groups, 2 * width, 2 * width), BF16),
            pltpu.VMEM((groups, 2 * width, 2 * width), BF16),
            pltpu.VMEM((lead, count, width), F32),
            pltpu.VMEM((lead, count, width), F32),
            pltpu.VMEM((lead, count, width), F32),
            pltpu.VMEM((count, width), F32),
            pltpu.VMEM((groups, count // groups, width), F32),
            pltpu.VMEM((lead, groups, 16, width), F32),
            pltpu.VMEM((groups, 16, width), F32),
            pltpu.VMEM((turns, lead, width), F32),
            pltpu.VMEM((turns, peers, lead, width), F32),
            pltpu.VMEM((ITERS + 1, count, width), F32),
            pltpu.VMEM((ITERS + 1, count, width), F32),
            pltpu.SemaphoreType.DMA((turns,)),
            pltpu.SemaphoreType.DMA((turns,)),
            pltpu.SemaphoreType.DMA(((ITERS + 1) * NCHUNK,)),
            pltpu.SemaphoreType.DMA(((ITERS + 1) * NCHUNK,)),
        ],
        compiler_params=pltpu.CompilerParams(collective_id=0, has_side_effects=True),
    )(
        initial,
        source,
        mix_rate.reshape(1, width),
        fine_inverse,
        coarse_inverse,
        step_counts.reshape(groups, count // groups),
    )


def solution(mesh):
    return jax.shard_map(
        body,
        mesh=mesh,
        in_specs=(
            P("cell", None),
            P("tm", "cell", None),
            P(),
            P("tm", "cell", None, None),
            P("tm", "cell", None, None),
            P("cell"),
        ),
        out_specs=P("tm", "cell", None),
        check_vma=False,
    )
```

time: 432 us -> 130 us (0.30)
  the two profiles are of different devices: /device:TPU:256 before, /device:TPU:448 now
where the time goes in v1:
time: 130 us
  Pallas kernels  128 us (98%)
  local copies, waits for them, and re-layouts  1.67 us (1%)
    pallas_call x1, Pallas kernels, body(): pl.pallas_call(kernel, out_shape=jax.ShapeDtypeStruct(source.shape, F32),...  128 us

profile of v1, /device:TPU:448, one launch (start us, length us, event | category | flops | bytes accessed | tf_op | source)
XLA Modules:
  0.0 130.0 jit_solution(10814444449846989711)
XLA Ops:
  0.0 128.3 %shard_map.64 = f32[2,256,128]{2,1,0:T(8,128)} custom-call(f32[256,128]{1,0:T(8,128)} %initial.1, f32[2,256,128]{2,1,0:T(8,128)} %source.1, f32[1,128]{1,0:T(1,128)} %bitcast.3, f32[2,2,128,128]{3,2,1,0:T(8,128)} %fine.1, f32[2,2,128,128]{3,2,1,0:T(8,128)} %coarse.1, s32[2,128]{1,0:T(2,128)} %bitcast.2), custom_call_target="tpu_custom_call" | custom-call | tf_op jit(solution)/shard_map/pallas_call | solution.py:240
  128.3 1.7 %copy.8 = f32[2,256,128]{2,1,0:T(8,128)} copy(f32[2,256,128]{2,1,0:T(8,128)} %shard_map.64) | data formatting | bytes 524288

commit v2 on v1

v2 whole, which is shorter than its diff:
```python
import jax
import jax.numpy as jnp
from jax import lax
from jax.experimental import pallas as pl
from jax.experimental.pallas import tpu as pltpu
from jax.sharding import PartitionSpec as P

FINE_MAX = 8
ITERS = 2
FEWEST = 4
CLASSES = 5
MESH = pl.DeviceIdType.MESH
F32 = jnp.float32
BF16 = jnp.bfloat16
XS, YS, CORES = 4, 8, 2
NCHUNK = 8


def split(a):
    high = a.astype(BF16)
    low = (a - high.astype(F32)).astype(BF16)
    return jnp.concatenate([high, low], axis=1)


def put_weights(ref, matrix):
    width = matrix.shape[0]
    pair = split(matrix)
    ref[0:width, :] = pair
    ref[width : 2 * width, :] = pair


def halves(a):
    width = a.shape[1] // 2
    return a[:, :width] + a[:, width:]


def mul(a, weights):
    return halves(jnp.dot(split(a), weights[...], preferred_element_type=F32))


def class_sums(onehot, cells):
    return halves(jnp.dot(onehot, split(cells), preferred_element_type=F32))


def pick(rows, counts):
    out = jnp.broadcast_to(rows[0:1], counts.shape)
    for j in range(1, CLASSES):
        out = jnp.where(counts == float(FEWEST + j), rows[j : j + 1], out)
    return out


def cell_place():
    me = lax.axis_index("cell")
    return me // (CORES * YS), (me // CORES) % YS, me % CORES


def cell_index(x, y, core):
    return (x * YS + y) * CORES + core


def farthest_first(xs, ys, cores):
    x, y, core = cell_place()
    moves = [
        (min(dx, XS - dx) + min(dy, YS - dy), dx, dy, dc)
        for dx in range(xs)
        for dy in range(ys)
        for dc in range(cores)
        if dx or dy or dc
    ]
    moves.sort(reverse=True)
    return [
        cell_index((x + dx) % XS, (y + dy) % YS, (core + dc) % CORES) for _, dx, dy, dc in moves
    ]


def total_rows(a):
    return jnp.sum(a, axis=0, keepdims=True)


def arrived(ref, sem):
    pltpu.make_async_copy(ref, ref, sem).wait()


def kernel(
    initial, source, mix, fine, coarse, steps, out,
    wf, wc, wp, wk, state, starts, off, shifted, counts, sums, weights_n,
    sbuf, rbuf, pair_s, pair_r, many_s, many_r, zs, zr,
    kl, kd, ks, kx, kr, ky, kf, kg, kall,
    ssem, rsem, pssem, prsem, mssem, mrsem, zssem, zrsem, kssem, krsem,
):
    lead, count, width = source.shape
    groups = fine.shape[1]
    per = count // groups
    tm = lax.axis_index("tm")
    last = lax.axis_size("tm") - 1
    x, y_at, core = cell_place()
    partner = cell_index(x, y_at, 1 - core)
    peers = farthest_first(XS, YS, CORES)
    far_peers = farthest_first(XS, YS, 1)
    cells = count * lax.axis_size("cell")
    chunk = count // NCHUNK
    slab = width // YS

    barrier = pltpu.get_barrier_semaphore()
    for peer in peers:
        pl.semaphore_signal(barrier, inc=1, device_id={"cell": peer}, device_id_type=MESH)
    behind = lax.rem(tm + last, last + 1)
    pl.semaphore_signal(barrier, inc=1, device_id={"tm": behind}, device_id_type=MESH)

    def rows(g):
        return pl.ds(g * per, per)

    def send(src, dst, ssem_one, rsem_one, peer):
        pltpu.make_async_remote_copy(
            src_ref=src,
            dst_ref=dst,
            send_sem=ssem_one,
            recv_sem=rsem_one,
            device_id={"cell": peer},
            device_id_type=MESH,
        ).start()

    rate = mix[...]
    keep = 1.0 - rate
    rate_down = jnp.broadcast_to(rate, (width, width)).T
    row_ids = lax.broadcasted_iota(jnp.int32, (8, width), 0)
    limits = jnp.concatenate([jnp.where(row_ids < CLASSES, row_ids + FEWEST, 0)] * 2, axis=0)
    onehots = []
    numbers = []
    for g in range(groups):
        for l in range(lead):
            put_weights(wf.at[l, g], fine[l, g])
            put_weights(wc.at[l, g], coarse[l, g])
        line = steps[g : g + 1, :]
        hot = jnp.where(line == row_ids + FEWEST, 1.0, 0.0).astype(F32)
        onehots.append(hot.astype(BF16))
        number = jnp.broadcast_to(jnp.sum(hot, axis=1, keepdims=True), (8, width))
        numbers.append(number)
        ones = jnp.where(row_ids < CLASSES, 1.0, 0.0).astype(F32)
        weights_n[g] = jnp.concatenate([number * rate, ones * rate], axis=0)
        counts[g] = jnp.broadcast_to(line.astype(F32), (per, width)).T
    for l in range(lead):
        for g in range(groups):
            over = 1.0 / cells
            six, seven = numbers[g][2:3] * over, (numbers[g][3:4] + numbers[g][4:5]) * over
            effect = rate_down * fine[l, g]
            terms = [(six + seven) * effect, seven * effect, six * effect, None]
            for d in range(4):
                terms.append(effect * (per * over))
                if d < 3:
                    effect = mul(effect * keep, wf.at[l, g])
                if d == 0:
                    terms[2] += seven * effect
            for i, term in enumerate(terms):
                if term is None:
                    kl[l, i] = jnp.zeros((width, width), F32)
                elif g == 0:
                    kl[l, i] = term
                else:
                    kl[l, i] += term
    for g in range(groups):
        put_weights(wp.at[g], mul(coarse[0, g], wc.at[1, g]))
        for l in range(lead):
            cells_l = source[l, rows(g)]
            summed = class_sums(onehots[g], cells_l)
            sums[l, g] = jnp.concatenate([summed, jnp.zeros_like(summed)], axis=0)
            off[l, rows(g)] = mul(cells_l, wc.at[l, g])
        shifted[rows(g)] = mul(off[0, rows(g)], wc.at[1, g]) + off[1, rows(g)]

    @pl.when(tm == 0)
    def _():
        for k in range(ITERS + 1):
            zr[k] = initial[...]

    pl.semaphore_wait(barrier, len(peers) + 1)

    def k_sems(stage, b):
        return kssem.at[stage * 2 + b], krsem.at[stage * 2 + b]

    def batch(b):
        return pl.ds(b * XS, XS)

    def pair_reduce_start(b):
        send(kl.at[1 - core, batch(b)], kd.at[batch(b)], *k_sems(0, b), partner)

    def x_reduce_start(b):
        arrived(kd.at[batch(b)], k_sems(0, b)[1])
        for i in range(XS):
            ks[b * XS + i] = kl[core, b * XS + i] + kd[b * XS + i]
        for slot, dx in enumerate((2, 1, 3)):
            to = (x + dx) % XS
            send(ks.at[b * XS + to], kx.at[b, slot], *k_sems(1, b), cell_index(to, y_at, core))

    def y_reduce_start(b):
        arrived(kx.at[b], k_sems(1, b)[1])
        kr[b] = ks[b * XS + x] + kx[b, 0] + kx[b, 1] + kx[b, 2]
        for slot, dy in enumerate((4, 3, 5, 2, 6, 1, 7)):
            to = (y_at + dy) % YS
            part = pl.ds(pl.multiple_of(to * slab, slab), slab)
            send(kr.at[b, part], ky.at[b, slot], *k_sems(2, b), cell_index(x, to, core))

    def y_gather_start(b):
        arrived(ky.at[b], k_sems(2, b)[1])
        part = pl.ds(pl.multiple_of(y_at * slab, slab), slab)
        piece = kr[b, part] + jnp.sum(ky[b], axis=0)
        kf[b] = piece
        kg[b, part] = piece
        for dy in (4, 3, 5, 2, 6, 1, 7):
            send(kf.at[b], kg.at[b, part], *k_sems(3, b), cell_index(x, (y_at + dy) % YS, core))

    def x_gather_start(b):
        arrived(ky.at[b], k_sems(3, b)[1])
        kall[core, b * XS + x] = kg[b]
        for dx in (2, 1, 3):
            send(
                kg.at[b], kall.at[core, b * XS + x], *k_sems(4, b),
                cell_index((x + dx) % XS, y_at, core),
            )

    def pair_gather_start(b):
        arrived(kx.at[b], k_sems(4, b)[1])
        send(kall.at[core, batch(b)], kall.at[core, batch(b)], *k_sems(5, b), partner)

    def k_finish(b):
        arrived(kall.at[1 - core, batch(b)], k_sems(5, b)[1])
        for l in range(lead):
            for i in range(XS):
                if b or i < 3:
                    put_weights(wk.at[l, b * XS + i], kall[l, b * XS + i])

    for b in range(2):
        pair_reduce_start(b)

    def hop(k, j):
        part = pl.ds(j * chunk, chunk)
        return pltpu.make_async_remote_copy(
            src_ref=zs.at[k, part],
            dst_ref=zr.at[k, part],
            send_sem=zssem.at[k * NCHUNK + j],
            recv_sem=zrsem.at[k * NCHUNK + j],
            device_id={"tm": lax.rem(tm + 1, last + 1)},
            device_id_type=MESH,
        )

    def chain(k):
        for j in range(NCHUNK):
            part = pl.ds(j * chunk, chunk)

            @pl.when(tm > 0)
            def _():
                hop(k, j).wait_recv()

            ending = mul(zr[k, part], wp.at[j * chunk // per]) + shifted[part]
            zs[k, part] = ending

            @pl.when(tm < last)
            def _():
                hop(k, j).start()

    def exchange_one(turn, own, work):
        sbuf[turn] = own
        for slot, peer in enumerate(peers):
            send(sbuf.at[turn], rbuf.at[turn, slot], ssem.at[turn], rsem.at[turn], peer)
        work()
        arrived(rbuf.at[turn], rsem.at[turn])
        return (own + jnp.sum(rbuf[turn], axis=0)) * (1.0 / cells)

    def exchange_many(turn, own, work):
        size = own.shape[0]
        part = pl.ds(0, size)
        pair_s[turn, part] = own
        send(pair_s.at[turn, part], pair_r.at[turn, part], pssem.at[turn], prsem.at[turn], partner)
        arrived(pair_r.at[turn, part], prsem.at[turn])
        both = own + pair_r[turn, part]
        many_s[turn, part] = both
        for slot, peer in enumerate(far_peers):
            send(
                many_s.at[turn, part], many_r.at[turn, slot, part],
                mssem.at[turn], mrsem.at[turn], peer,
            )
        work()
        whole = many_r.at[turn, pl.ds(0, len(far_peers)), part]
        arrived(whole, mrsem.at[turn])
        return (both + jnp.sum(many_r[turn, :, part], axis=0)) * (1.0 / cells)

    def partial(y, l):
        return total_rows(sum(y[l, g][0:8] for g in range(groups)))

    def advance(y, m, average):
        made = {}
        for l in range(lead):
            for g in range(groups):
                old = y[l, g]
                fed = old * keep + sums[l, g, 0 : old.shape[0]]
                if average is not None:
                    fed = fed + weights_n[g] * average[l]
                new = mul(fed, wf.at[l, g])
                made[l, g] = jnp.where(limits[0 : old.shape[0]] > m, new, old) if m >= FEWEST else new
        return made

    def fine_cells(m):
        for l in range(lead):
            for g in range(groups):
                old = state[l, rows(g)]
                new = mul(old * keep + source[l, rows(g)], wf.at[l, g])
                if m >= FEWEST:
                    new = jnp.where(counts[g] > float(m), new, old)
                state[l, rows(g)] = new

    def offsets(it):
        for g in range(groups):
            for l in range(lead):
                begin = zr[it, rows(g)] if l == 0 else starts[1, rows(g)]
                off[l, rows(g)] = state[l, rows(g)] - mul(begin, wc.at[l, g])
            shifted[rows(g)] = mul(off[0, rows(g)], wc.at[1, g]) + off[1, rows(g)]

    def through(row, l, i):
        return mul(jnp.broadcast_to(row, (8, width)), wk.at[l, i])[0:1]

    def begin(it):
        y = {}
        for g in range(groups):
            first = zr[it, rows(g)]
            second = mul(first, wc.at[0, g]) + off[0, rows(g)]
            starts[1, rows(g)] = second
            for l, cells_l in ((0, first), (1, second)):
                state[l, rows(g)] = cells_l
                summed = class_sums(onehots[g], cells_l)
                y[l, g] = jnp.concatenate([summed, jnp.zeros_like(summed)], axis=0)
        return y

    def late(y, turn, work):
        free = [y]
        for m in (5, 6):
            tops = {k: v[0:8] for k, v in free[-1].items()}
            free.append(advance(tops, m, None))
        own = jnp.concatenate([partial(f, l) for l in range(lead) for f in free], axis=0)
        got = exchange_many(turn, own, work)
        fifth = [got[3 * l : 3 * l + 1] for l in range(lead)]
        y = advance(y, 5, fifth)
        sixth = [got[3 * l + 1 : 3 * l + 2] + through(fifth[l], l, 0) for l in range(lead)]
        seventh = [got[3 * l + 2 : 3 * l + 3] + through(fifth[l], l, 2) for l in range(lead)]
        y = advance(y, 6, sixth)
        seventh = [seventh[l] + through(sixth[l], l, 1) for l in range(lead)]
        return advance(y, 7, seventh)

    def finish(y, it):
        for g in range(groups):
            extra = mul(y[0, g], wc.at[1, g]) + y[1, g]
            shifted[rows(g)] += pick(extra[8:16], counts[g])
        chain(it + 1)
        for g in range(groups):
            off[0, rows(g)] += pick(y[0, g][8:16], counts[g])

    chain(0)
    y = begin(0)

    def beside(m):
        def work():
            if m < 4:
                fine_cells(2 * m)
                fine_cells(2 * m + 1)
            if m == 0:
                x_reduce_start(0)
            elif m == 1:
                y_reduce_start(0)
                x_reduce_start(1)
            elif m == 2:
                y_gather_start(0)
            elif m == 3:
                x_gather_start(0)
                y_reduce_start(1)
            elif m == 4:
                offsets(0)
                pair_gather_start(0)
                y_gather_start(1)
            else:
                k_finish(0)
                x_gather_start(1)

        return work

    for m in range(5):
        own = jnp.concatenate([partial(y, l) for l in range(lead)], axis=0)
        average = exchange_one(m, own, beside(m))
        y = advance(y, m, [average[l : l + 1] for l in range(lead)])
    y = late(y, 0, beside(5))
    finish(y, 0)

    y = begin(1)
    free = [{k: v[0:8] for k, v in y.items()}]
    for m in range(4):
        free.append(advance(free[-1], m, None))
    own = jnp.concatenate([partial(f, l) for l in range(lead) for f in free], axis=0)

    def work():
        pair_gather_start(1)
        for m in range(FINE_MAX):
            fine_cells(m)
        k_finish(1)

    got = exchange_many(1, own, work)
    averages = [[got[5 * l + m : 5 * l + m + 1] for m in range(5)] for l in range(lead)]
    for m in range(4):
        for l in range(lead):
            for later in range(m + 1, 5):
                averages[l][later] += through(averages[l][m], l, XS + later - m - 1)
    for m in range(5):
        y = advance(y, m, [averages[l][m] for l in range(lead)])
    y = late(y, 2, lambda: offsets(1))
    finish(y, 1)

    for g in range(groups):
        out[0, rows(g)] = mul(zr[ITERS, rows(g)], wc.at[0, g]) + off[0, rows(g)]
        out[1, rows(g)] = zs[ITERS, rows(g)]

    def drain(turn, carry):
        arrived(rbuf.at[turn], ssem.at[turn])
        return carry

    lax.fori_loop(0, 5, drain, 0)
    for turn, size in ((0, 6), (1, 10), (2, 6)):
        part = pl.ds(0, size)
        arrived(pair_s.at[turn, part], pssem.at[turn])
        arrived(many_r.at[turn, pl.ds(0, len(far_peers)), part], mssem.at[turn])
    for b in range(2):
        for stage, ref in enumerate((kd.at[batch(b)], kx.at[b], ky.at[b], ky.at[b], kx.at[b], kd.at[batch(b)])):
            arrived(ref, k_sems(stage, b)[0])

    @pl.when(tm < last)
    def _():
        for k in range(ITERS + 1):
            for j in range(NCHUNK):
                hop(k, j).wait_send()


def body(initial, source, mix_rate, fine_inverse, coarse_inverse, step_counts):
    lead, count, width = source.shape
    groups = fine_inverse.shape[1]
    peers = XS * YS * CORES - 1
    far = XS * YS - 1
    mats = 2 * XS
    vmem = pl.BlockSpec(memory_space=pltpu.VMEM)
    return pl.pallas_call(
        kernel,
        out_shape=jax.ShapeDtypeStruct(source.shape, F32),
        in_specs=[vmem] * 6,
        out_specs=vmem,
        scratch_shapes=[
            pltpu.VMEM((lead, groups, 2 * width, 2 * width), BF16),
            pltpu.VMEM((lead, groups, 2 * width, 2 * width), BF16),
            pltpu.VMEM((groups, 2 * width, 2 * width), BF16),
            pltpu.VMEM((lead, mats, 2 * width, 2 * width), BF16),
            pltpu.VMEM((lead, count, width), F32),
            pltpu.VMEM((lead, count, width), F32),
            pltpu.VMEM((lead, count, width), F32),
            pltpu.VMEM((count, width), F32),
            pltpu.VMEM((groups, count // groups, width), F32),
            pltpu.VMEM((lead, groups, 16, width), F32),
            pltpu.VMEM((groups, 16, width), F32),
            pltpu.VMEM((5, lead, width), F32),
            pltpu.VMEM((5, peers, lead, width), F32),
            pltpu.VMEM((3, 16, width), F32),
            pltpu.VMEM((3, 16, width), F32),
            pltpu.VMEM((3, 16, width), F32),
            pltpu.VMEM((3, far, 16, width), F32),
            pltpu.VMEM((ITERS + 1, count, width), F32),
            pltpu.VMEM((ITERS + 1, count, width), F32),
            pltpu.VMEM((lead, mats, width, width), F32),
            pltpu.VMEM((mats, width, width), F32),
            pltpu.VMEM((mats, width, width), F32),
            pltpu.VMEM((2, XS - 1, width, width), F32),
            pltpu.VMEM((2, width, width), F32),
            pltpu.VMEM((2, YS - 1, width // YS, width), F32),
            pltpu.VMEM((2, width // YS, width), F32),
            pltpu.VMEM((2, width, width), F32),
            pltpu.VMEM((lead, mats, width, width), F32),
            pltpu.SemaphoreType.DMA((5,)),
            pltpu.SemaphoreType.DMA((5,)),
            pltpu.SemaphoreType.DMA((3,)),
            pltpu.SemaphoreType.DMA((3,)),
            pltpu.SemaphoreType.DMA((3,)),
            pltpu.SemaphoreType.DMA((3,)),
            pltpu.SemaphoreType.DMA(((ITERS + 1) * NCHUNK,)),
            pltpu.SemaphoreType.DMA(((ITERS + 1) * NCHUNK,)),
            pltpu.SemaphoreType.DMA((12,)),
            pltpu.SemaphoreType.DMA((12,)),
        ],
        compiler_params=pltpu.CompilerParams(collective_id=0, has_side_effects=True),
    )(
        initial,
        source,
        mix_rate.reshape(1, width),
        fine_inverse,
        coarse_inverse,
        step_counts.reshape(groups, count // groups),
    )


def solution(mesh):
    return jax.shard_map(
        body,
        mesh=mesh,
        in_specs=(
            P("cell", None),
            P("tm", "cell", None),
            P(),
            P("tm", "cell", None, None),
            P("tm", "cell", None, None),
            P("cell"),
        ),
        out_specs=P("tm", "cell", None),
        check_vma=False,
    )
```

time: 130 us -> 89.2 us (0.69)
  Pallas kernels: 128 us -> 87.4 us
    pallas_call x1, Pallas kernels: 128 us -> 87.4 us  [body(): pl.pallas_call(kernel, out_shape=jax.ShapeDtypeStruct(source.shape, F32),...]
where the time goes in v2:
time: 89.2 us; the launch traced here: 89 us
  Pallas kernels  87.4 us (98%)
  local copies, waits for them, and re-layouts  1.67 us (2%)
    pallas_call x1, Pallas kernels, body(): pl.pallas_call(kernel, out_shape=jax.ShapeDtypeStruct(source.shape, F32),...  87.4 us

profile of v2, /device:TPU:448, one launch (start us, length us, event | category | flops | bytes accessed | tf_op | source)
XLA Modules:
  0.0 89.0 jit_solution(11752546318909423849)
XLA Ops:
  0.0 87.4 %shard_map.64 = f32[2,256,128]{2,1,0:T(8,128)} custom-call(f32[256,128]{1,0:T(8,128)} %initial.1, f32[2,256,128]{2,1,0:T(8,128)} %source.1, f32[1,128]{1,0:T(1,128)} %bitcast.3, f32[2,2,128,128]{3,2,1,0:T(8,128)} %fine.1, f32[2,2,128,128]{3,2,1,0:T(8,128)} %coarse.1, s32[2,128]{1,0:T(2,128)} %bitcast.2), custom_call_target="tpu_custom_call" | custom-call | tf_op jit(solution)/shard_map/pallas_call | solution.py:444
  87.4 1.7 %copy.8 = f32[2,256,128]{2,1,0:T(8,128)} copy(f32[2,256,128]{2,1,0:T(8,128)} %shard_map.64) | data formatting | bytes 524288

commit v3 on v2

v3 whole, which is shorter than its diff:
```python
import jax
import jax.numpy as jnp
from jax import lax
from jax.experimental import pallas as pl
from jax.experimental.pallas import tpu as pltpu
from jax.sharding import PartitionSpec as P

FINE_MAX = 8
ITERS = 2
FEWEST = 4
CLASSES = 5
MESH = pl.DeviceIdType.MESH
F32 = jnp.float32
BF16 = jnp.bfloat16
XS, YS, CORES = 4, 8, 2
NCHUNK = 8


def split(a):
    high = a.astype(BF16)
    low = (a - high.astype(F32)).astype(BF16)
    return jnp.concatenate([high, low], axis=1)


def put_weights(ref, matrix):
    width = matrix.shape[0]
    pair = split(matrix)
    ref[0:width, :] = pair
    ref[width : 2 * width, :] = pair


def halves(a):
    width = a.shape[1] // 2
    return a[:, :width] + a[:, width:]


def mul(a, weights):
    return halves(jnp.dot(split(a), weights[...], preferred_element_type=F32))


def class_sums(onehot, cells):
    return halves(jnp.dot(onehot, split(cells), preferred_element_type=F32))


def pick(rows, counts):
    out = jnp.broadcast_to(rows[CLASSES : CLASSES + 1], counts.shape)
    for j in range(1, CLASSES):
        out = jnp.where(counts == float(FEWEST + j), rows[CLASSES + j : CLASSES + j + 1], out)
    return out


def cell_place():
    me = lax.axis_index("cell")
    return me // (CORES * YS), (me // CORES) % YS, me % CORES


def cell_index(x, y, core):
    return (x * YS + y) * CORES + core


def farthest_first(xs, ys, cores):
    x, y, core = cell_place()
    moves = [
        (min(dx, XS - dx) + min(dy, YS - dy), dx, dy, dc)
        for dx in range(xs)
        for dy in range(ys)
        for dc in range(cores)
        if dx or dy or dc
    ]
    moves.sort(reverse=True)
    return [
        cell_index((x + dx) % XS, (y + dy) % YS, (core + dc) % CORES) for _, dx, dy, dc in moves
    ]


def total_rows(a):
    return jnp.sum(a, axis=0, keepdims=True)


def arrived(ref, sem):
    pltpu.make_async_copy(ref, ref, sem).wait()


def kernel(
    initial, source, mix, fine, coarse, steps, out,
    wf, wc, wp, wk, state, starts, off, shifted, counts, sums, weights_n, yinit,
    fine_p, coarse_p, begun, offy, sbuf, rbuf, many_s, many_r, zs, zr, ys, yr, fin, fin_p,
    kl, kd, ks, kx, kr, ky, kf, kg, kall,
    ssem, rsem, mssem, mrsem, zssem, zrsem, yssem, yrsem, kssem, krsem, pssem, prsem,
):
    lead, count, width = source.shape
    groups = fine.shape[1]
    every = 2 * groups
    per = count // groups
    tm = lax.axis_index("tm")
    last = lax.axis_size("tm") - 1
    x, y_at, core = cell_place()
    partner = cell_index(x, y_at, 1 - core)
    far_peers = farthest_first(XS, YS, 1)
    x_moves, y_moves = (2, 1, 3), (4, 3, 5, 2, 6, 1, 7)
    cells = count * lax.axis_size("cell")
    chunk = count // NCHUNK
    slab = width // YS
    used = 2 * CLASSES
    lead_core = core == 1

    barrier = pltpu.get_barrier_semaphore()

    def greet(peer):
        pl.semaphore_signal(barrier, inc=1, device_id={"cell": peer}, device_id_type=MESH)

    @pl.when(lead_core)
    def _():
        for peer in far_peers:
            greet(peer)

    @pl.when(jnp.logical_not(lead_core))
    def _():
        for d in x_moves:
            greet(cell_index((x + d) % XS, y_at, core))
        for d in y_moves:
            greet(cell_index(x, (y_at + d) % YS, core))

    greet(partner)
    behind = lax.rem(tm + last, last + 1)
    pl.semaphore_signal(barrier, inc=1, device_id={"tm": behind}, device_id_type=MESH)

    def rows(g):
        return pl.ds(g * per, per)

    def send(src, dst, ssem_one, rsem_one, peer):
        pltpu.make_async_remote_copy(
            src_ref=src,
            dst_ref=dst,
            send_sem=ssem_one,
            recv_sem=rsem_one,
            device_id={"cell": peer},
            device_id_type=MESH,
        ).start()

    rate = mix[...]
    keep = 1.0 - rate
    rate_down = jnp.broadcast_to(rate, (width, width)).T
    row_ids = lax.broadcasted_iota(jnp.int32, (16, width), 0)
    cell_row = row_ids[0:8] < CLASSES
    limits = jnp.where(
        row_ids < CLASSES, row_ids + FEWEST, jnp.where(row_ids < used, row_ids + FEWEST - CLASSES, 0)
    )
    shared = jnp.where(jnp.logical_and(row_ids >= CLASSES, row_ids < used), 1.0, 0.0).astype(F32)

    def padded(a):
        return jnp.concatenate([a, jnp.zeros_like(a)], axis=0)

    numbers = []
    for g in range(groups):
        for l in range(lead):
            put_weights(wf.at[l, g], fine[l, g])
            put_weights(wc.at[l, g], coarse[l, g])
        line = steps[g : g + 1, :]
        hot = jnp.where(
            jnp.logical_and(line == row_ids[0:8] + FEWEST, cell_row), 1.0, 0.0
        ).astype(F32)
        onehot = hot.astype(BF16)
        number = jnp.broadcast_to(jnp.sum(hot, axis=1, keepdims=True), (8, width))
        numbers.append(number)
        weights_n[g] = (padded(number) + shared) * rate
        counts[g] = jnp.broadcast_to(line.astype(F32), (per, width)).T
        yinit[g] = padded(class_sums(onehot, initial[rows(g)]))
        for l in range(lead):
            sums[l, g] = padded(class_sums(onehot, source[l, rows(g)]))

    def bulk_setup():
        for g in range(groups):
            put_weights(wp.at[g], mul(coarse[0, g], wc.at[1, g]))
            for l in range(lead):
                off[l, rows(g)] = mul(source[l, rows(g)], wc.at[l, g])
            shifted[rows(g)] = mul(off[0, rows(g)], wc.at[1, g]) + off[1, rows(g)]

    def condense():
        over = 1.0 / cells
        for l in range(lead):
            for g in range(groups):
                six, seven = numbers[g][2:3] * over, (numbers[g][3:4] + numbers[g][4:5]) * over
                effect = rate_down * fine[l, g]
                terms = [(six + seven) * effect, seven * effect, six * effect, None]
                for d in range(4):
                    terms.append(effect * (per * over))
                    if d < 3:
                        effect = mul(effect * keep, wf.at[l, g])
                    if d == 0:
                        terms[2] += seven * effect
                for i, term in enumerate(terms):
                    if term is None:
                        kl[l, i] = jnp.zeros((width, width), F32)
                    elif g == 0:
                        kl[l, i] = term
                    else:
                        kl[l, i] += term

    @pl.when(tm == 0)
    def _():
        for k in range(ITERS + 1):
            zr[k] = initial[...]

    def k_sems(stage, b):
        return kssem.at[stage * 2 + b], krsem.at[stage * 2 + b]

    def batch(b):
        return pl.ds(b * XS, XS)

    def pair_reduce_start(b):
        send(kl.at[1 - core, batch(b)], kd.at[batch(b)], *k_sems(0, b), partner)

    def x_reduce_start(b):
        arrived(kd.at[batch(b)], k_sems(0, b)[1])
        for i in range(XS):
            ks[b * XS + i] = kl[core, b * XS + i] + kd[b * XS + i]
        for slot, dx in enumerate(x_moves):
            to = (x + dx) % XS
            send(ks.at[b * XS + to], kx.at[b, slot], *k_sems(1, b), cell_index(to, y_at, core))

    def y_reduce_start(b):
        arrived(kx.at[b], k_sems(1, b)[1])
        kr[b] = ks[b * XS + x] + kx[b, 0] + kx[b, 1] + kx[b, 2]
        for slot, dy in enumerate(y_moves):
            to = (y_at + dy) % YS
            part = pl.ds(pl.multiple_of(to * slab, slab), slab)
            send(kr.at[b, part], ky.at[b, slot], *k_sems(2, b), cell_index(x, to, core))

    def y_gather_start(b):
        arrived(ky.at[b], k_sems(2, b)[1])
        part = pl.ds(pl.multiple_of(y_at * slab, slab), slab)
        piece = kr[b, part] + jnp.sum(ky[b], axis=0)
        kf[b] = piece
        kg[b, part] = piece
        for dy in y_moves:
            send(kf.at[b], kg.at[b, part], *k_sems(3, b), cell_index(x, (y_at + dy) % YS, core))

    def x_gather_start(b):
        arrived(ky.at[b], k_sems(3, b)[1])
        kall[core, b * XS + x] = kg[b]
        for dx in x_moves:
            send(
                kg.at[b], kall.at[core, b * XS + x], *k_sems(4, b),
                cell_index((x + dx) % XS, y_at, core),
            )

    def x_gather_done(b):
        arrived(kx.at[b], k_sems(4, b)[1])

    def pair_gather_start(b):
        x_gather_done(b)
        send(kall.at[core, batch(b)], kall.at[core, batch(b)], *k_sems(5, b), partner)

    def k_finish(b):
        arrived(kall.at[1 - core, batch(b)], k_sems(5, b)[1])
        for l in range(lead):
            for i in range(XS):
                if b or i < 3:
                    put_weights(wk.at[l, b * XS + i], kall[l, b * XS + i])

    def hop(k, j):
        part = pl.ds(j * chunk, chunk)
        return pltpu.make_async_remote_copy(
            src_ref=zs.at[k, part],
            dst_ref=zr.at[k, part],
            send_sem=zssem.at[k * NCHUNK + j],
            recv_sem=zrsem.at[k * NCHUNK + j],
            device_id={"tm": lax.rem(tm + 1, last + 1)},
            device_id_type=MESH,
        )

    def bulk_chain(k):
        for j in range(NCHUNK):
            part = pl.ds(j * chunk, chunk)

            @pl.when(tm > 0)
            def _():
                hop(k, j).wait_recv()

            zs[k, part] = mul(zr[k, part], wp.at[j * chunk // per]) + shifted[part]

            @pl.when(tm < last)
            def _():
                hop(k, j).start()

    def bulk_begin(it):
        for g in range(groups):
            first = zr[it, rows(g)]
            second = mul(first, wc.at[0, g]) + off[0, rows(g)]
            starts[1, rows(g)] = second
            state[0, rows(g)] = first
            state[1, rows(g)] = second

    def fine_cells(m):
        for l in range(lead):
            for g in range(groups):
                old = state[l, rows(g)]
                new = mul(old * keep + source[l, rows(g)], wf.at[l, g])
                if m >= FEWEST:
                    new = jnp.where(counts[g] > float(m), new, old)
                state[l, rows(g)] = new

    def bulk_offsets(it):
        for g in range(groups):
            for l in range(lead):
                begin = zr[it, rows(g)] if l == 0 else starts[1, rows(g)]
                off[l, rows(g)] = state[l, rows(g)] - mul(begin, wc.at[l, g])
            shifted[rows(g)] = mul(off[0, rows(g)], wc.at[1, g]) + off[1, rows(g)]

    def bulk_result():
        for g in range(groups):
            state[0, rows(g)] = mul(zr[ITERS, rows(g)], wc.at[0, g]) + off[0, rows(g)]

    def result(rows_of):
        for g in range(groups):
            out[0, rows(g)] = state[0, rows(g)] + pick(rows_of(0, g), counts[g])
            out[1, rows(g)] = zs[ITERS, rows(g)] + pick(rows_of(1, g), counts[g])

    def drain_common():
        for b in range(2):
            for stage, ref in enumerate((kd.at[batch(b)], kx.at[b], ky.at[b], ky.at[b], kx.at[b])):
                arrived(ref, k_sems(stage, b)[0])

        @pl.when(tm < last)
        def _():
            for k in range(ITERS + 1):
                for j in range(NCHUNK):
                    hop(k, j).wait_send()

    own_groups, partner_groups = pl.ds(0, groups), pl.ds(groups, groups)

    def shared_copies():
        pairs = [
            (fine, fine_p),
            (coarse, coarse_p),
            (weights_n.at[own_groups], weights_n.at[partner_groups]),
            (yinit.at[own_groups], yinit.at[partner_groups]),
        ]
        pairs += [(sums.at[l, own_groups], sums.at[l, partner_groups]) for l in range(lead)]
        return pairs

    @pl.when(jnp.logical_not(lead_core))
    def _():
        condense()
        pl.semaphore_wait(barrier, len(x_moves) + len(y_moves) + 2)
        for i, (src, dst) in enumerate(shared_copies()):
            send(src, dst, pssem.at[i], prsem.at[i], partner)
        pair_reduce_start(0)
        pair_reduce_start(1)
        bulk_setup()
        x_reduce_start(0)
        x_reduce_start(1)
        y_reduce_start(0)
        bulk_chain(0)
        bulk_begin(0)
        y_gather_start(0)
        for m in range(4):
            fine_cells(m)
        y_reduce_start(1)
        x_gather_start(0)
        for m in range(4, FINE_MAX):
            fine_cells(m)
        y_gather_start(1)
        pair_gather_start(0)
        bulk_offsets(0)
        x_gather_start(1)
        bulk_chain(1)
        bulk_begin(1)
        pair_gather_start(1)
        for m in range(FINE_MAX):
            fine_cells(m)
        bulk_offsets(1)
        bulk_chain(2)
        bulk_result()
        arrived(fin_p, prsem.at[7])
        result(lambda l, g: fin_p[l, g])
        for i, (src, _) in enumerate(shared_copies()):
            arrived(src, pssem.at[i])
        for b in range(2):
            arrived(kd.at[batch(b)], k_sems(5, b)[0])
        drain_common()

    @pl.when(lead_core)
    def _():
        condense()
        bulk_setup()
        pl.semaphore_wait(barrier, len(far_peers) + 2)
        pair_reduce_start(0)
        pair_reduce_start(1)
        for i, (_, dst) in enumerate(shared_copies()):
            arrived(dst, prsem.at[i])
        for g in range(groups):
            for l in range(lead):
                put_weights(wf.at[l, groups + g], fine_p[l, g])
                put_weights(wc.at[l, groups + g], coarse_p[l, g])
            put_weights(wp.at[groups + g], mul(coarse_p[0, g], wc.at[1, groups + g]))

        @pl.when(tm == 0)
        def _():
            for k in range(ITERS + 1):
                yr[k] = yinit[...]

        each = [(l, g) for l in range(lead) for g in range(every)]
        used_rows = pl.ds(0, used)

        def row_hop(k):
            return pltpu.make_async_remote_copy(
                src_ref=ys.at[k, :, used_rows],
                dst_ref=yr.at[k, :, used_rows],
                send_sem=yssem.at[k],
                recv_sem=yrsem.at[k],
                device_id={"tm": lax.rem(tm + 1, last + 1)},
                device_id_type=MESH,
            )

        def row_chain(k):
            step = [mul(offy[0, g], wc.at[1, g]) + offy[1, g] for g in range(every)]

            @pl.when(tm > 0)
            def _():
                row_hop(k).wait_recv()

            for g in range(every):
                ys[k, g] = mul(yr[k, g], wp.at[g]) + step[g]

            @pl.when(tm < last)
            def _():
                row_hop(k).start()

        def row_begin(k):
            y = {}
            for g in range(every):
                y[0, g] = yr[k, g]
                y[1, g] = mul(yr[k, g], wc.at[0, g]) + offy[0, g]
            for l, g in each:
                begun[l, g] = y[l, g]
            return y

        def row_coarse():
            for l, g in each:
                begun[l, g] = mul(begun[l, g], wc.at[l, g])

        def row_offsets(y):
            for l, g in each:
                offy[l, g] = y[l, g] - begun[l, g]

        def exchange_one(turn, own, work):
            sbuf[turn] = own
            for slot, peer in enumerate(far_peers):
                send(sbuf.at[turn], rbuf.at[turn, slot], ssem.at[turn], rsem.at[turn], peer)
            work()
            arrived(rbuf.at[turn], rsem.at[turn])
            return (own + jnp.sum(rbuf[turn], axis=0)) * (1.0 / cells)

        def exchange_many(turn, own, work):
            part = pl.ds(0, own.shape[0])
            many_s[turn, part] = own
            for slot, peer in enumerate(far_peers):
                send(
                    many_s.at[turn, part], many_r.at[turn, slot, part],
                    mssem.at[turn], mrsem.at[turn], peer,
                )
            work()
            arrived(many_r.at[turn, :, part], mrsem.at[turn])
            return (own + jnp.sum(many_r[turn, :, part], axis=0)) * (1.0 / cells)

        def partial(y, l):
            return total_rows(jnp.where(cell_row, sum(y[l, g][0:8] for g in range(every)), 0.0))

        def advance(y, m, average):
            made = {}
            for l, g in each:
                old = y[l, g]
                size = old.shape[0]
                fed = old * keep + sums[l, g, 0:size]
                if average is not None:
                    fed = fed + weights_n[g] * average[l]
                new = mul(fed, wf.at[l, g])
                made[l, g] = jnp.where(limits[0:size] > m, new, old) if m >= FEWEST else new
            return made

        def through(row, l, i):
            return mul(jnp.broadcast_to(row, (8, width)), wk.at[l, i])[0:1]

        def late(y, turn, work):
            free = [y]
            for m in (5, 6):
                tops = {k: v[0:8] for k, v in free[-1].items()}
                free.append(advance(tops, m, None))
            own = jnp.concatenate([partial(f, l) for l in range(lead) for f in free], axis=0)
            got = exchange_many(turn, own, work)
            fifth = [got[3 * l : 3 * l + 1] for l in range(lead)]
            y = advance(y, 5, fifth)
            sixth = [got[3 * l + 1 : 3 * l + 2] + through(fifth[l], l, 0) for l in range(lead)]
            seventh = [got[3 * l + 2 : 3 * l + 3] + through(fifth[l], l, 2) for l in range(lead)]
            y = advance(y, 6, sixth)
            seventh = [seventh[l] + through(sixth[l], l, 1) for l in range(lead)]
            return advance(y, 7, seventh)

        for l, g in each:
            offy[l, g] = mul(sums[l, g], wc.at[l, g])
        row_chain(0)
        y = row_begin(0)

        def beside(m):
            def work():
                if m == 0:
                    x_reduce_start(0)
                    row_coarse()
                elif m == 1:
                    y_reduce_start(0)
                    x_reduce_start(1)
                    bulk_chain(0)
                elif m == 2:
                    y_gather_start(0)
                    bulk_begin(0)
                    for i in range(4):
                        fine_cells(i)
                elif m == 3:
                    x_gather_start(0)
                    y_reduce_start(1)
                    for i in range(4, FINE_MAX):
                        fine_cells(i)
                elif m == 4:
                    y_gather_start(1)
                    x_gather_done(0)
                    bulk_offsets(0)
                else:
                    x_gather_start(1)
                    bulk_chain(1)
                    k_finish(0)

            return work

        for m in range(5):
            own = jnp.concatenate([partial(y, l) for l in range(lead)], axis=0)
            average = exchange_one(m, own, beside(m))
            y = advance(y, m, [average[l : l + 1] for l in range(lead)])
        row_offsets(late(y, 0, beside(5)))
        row_chain(1)

        y = row_begin(1)
        free = [{k: v[0:8] for k, v in y.items()}]
        for m in range(4):
            free.append(advance(free[-1], m, None))
        own = jnp.concatenate([partial(f, l) for l in range(lead) for f in free], axis=0)

        def work():
            row_coarse()
            bulk_begin(1)
            for m in range(FINE_MAX):
                fine_cells(m)
            x_gather_done(1)
            k_finish(1)

        got = exchange_many(1, own, work)
        averages = [[got[5 * l + m : 5 * l + m + 1] for m in range(5)] for l in range(lead)]
        for m in range(4):
            for l in range(lead):
                for later in range(m + 1, 5):
                    averages[l][later] += through(averages[l][m], l, XS + later - m - 1)
        for m in range(5):
            y = advance(y, m, [averages[l][m] for l in range(lead)])

        def work():
            bulk_offsets(1)
            bulk_chain(2)
            bulk_result()

        row_offsets(late(y, 2, work))
        row_chain(2)
        for g in range(every):
            fin[0, g] = mul(yr[ITERS, g], wc.at[0, g]) + offy[0, g]
            fin[1, g] = ys[ITERS, g]
        for l in range(lead):
            send(fin.at[l, partner_groups], fin_p.at[l], pssem.at[6 + l], prsem.at[7], partner)
        result(lambda l, g: fin[l, g])

        for turn in range(5):
            arrived(rbuf.at[turn], ssem.at[turn])
        for turn, size in ((0, 6), (1, 10), (2, 6)):
            arrived(many_r.at[turn, :, pl.ds(0, size)], mssem.at[turn])
        for l in range(lead):
            arrived(fin_p.at[l], pssem.at[6 + l])
        drain_common()

        @pl.when(tm < last)
        def _():
            for k in range(ITERS + 1):
                row_hop(k).wait_send()


def body(initial, source, mix_rate, fine_inverse, coarse_inverse, step_counts):
    lead, count, width = source.shape
    groups = fine_inverse.shape[1]
    every = 2 * groups
    far = XS * YS - 1
    mats = 2 * XS
    vmem = pl.BlockSpec(memory_space=pltpu.VMEM)
    return pl.pallas_call(
        kernel,
        out_shape=jax.ShapeDtypeStruct(source.shape, F32),
        in_specs=[vmem] * 6,
        out_specs=vmem,
        scratch_shapes=[
            pltpu.VMEM((lead, every, 2 * width, 2 * width), BF16),
            pltpu.VMEM((lead, every, 2 * width, 2 * width), BF16),
            pltpu.VMEM((every, 2 * width, 2 * width), BF16),
            pltpu.VMEM((lead, mats, 2 * width, 2 * width), BF16),
            pltpu.VMEM((lead, count, width), F32),
            pltpu.VMEM((lead, count, width), F32),
            pltpu.VMEM((lead, count, width), F32),
            pltpu.VMEM((count, width), F32),
            pltpu.VMEM((groups, count // groups, width), F32),
            pltpu.VMEM((lead, every, 16, width), F32),
            pltpu.VMEM((every, 16, width), F32),
            pltpu.VMEM((every, 16, width), F32),
            pltpu.VMEM((lead, groups, width, width), F32),
            pltpu.VMEM((lead, groups, width, width), F32),
            pltpu.VMEM((lead, every, 16, width), F32),
            pltpu.VMEM((lead, every, 16, width), F32),
            pltpu.VMEM((5, lead, width), F32),
            pltpu.VMEM((5, far, lead, width), F32),
            pltpu.VMEM((3, 16, width), F32),
            pltpu.VMEM((3, far, 16, width), F32),
            pltpu.VMEM((ITERS + 1, count, width), F32),
            pltpu.VMEM((ITERS + 1, count, width), F32),
            pltpu.VMEM((ITERS + 1, every, 16, width), F32),
            pltpu.VMEM((ITERS + 1, every, 16, width), F32),
            pltpu.VMEM((lead, every, 16, width), F32),
            pltpu.VMEM((lead, groups, 16, width), F32),
            pltpu.VMEM((lead, mats, width, width), F32),
            pltpu.VMEM((mats, width, width), F32),
            pltpu.VMEM((mats, width, width), F32),
            pltpu.VMEM((2, XS - 1, width, width), F32),
            pltpu.VMEM((2, width, width), F32),
            pltpu.VMEM((2, YS - 1, width // YS, width), F32),
            pltpu.VMEM((2, width // YS, width), F32),
            pltpu.VMEM((2, width, width), F32),
            pltpu.VMEM((lead, mats, width, width), F32),
            pltpu.SemaphoreType.DMA((5,)),
            pltpu.SemaphoreType.DMA((5,)),
            pltpu.SemaphoreType.DMA((3,)),
            pltpu.SemaphoreType.DMA((3,)),
            pltpu.SemaphoreType.DMA(((ITERS + 1) * NCHUNK,)),
            pltpu.SemaphoreType.DMA(((ITERS + 1) * NCHUNK,)),
            pltpu.SemaphoreType.DMA((ITERS + 1,)),
            pltpu.SemaphoreType.DMA((ITERS + 1,)),
            pltpu.SemaphoreType.DMA((12,)),
            pltpu.SemaphoreType.DMA((12,)),
            pltpu.SemaphoreType.DMA((8,)),
            pltpu.SemaphoreType.DMA((8,)),
        ],
        compiler_params=pltpu.CompilerParams(collective_id=0, has_side_effects=True),
    )(
        initial,
        source,
        mix_rate.reshape(1, width),
        fine_inverse,
        coarse_inverse,
        step_counts.reshape(groups, count // groups),
    )


def solution(mesh):
    return jax.shard_map(
        body,
        mesh=mesh,
        in_specs=(
            P("cell", None),
            P("tm", "cell", None),
            P(),
            P("tm", "cell", None, None),
            P("tm", "cell", None, None),
            P("cell"),
        ),
        out_specs=P("tm", "cell", None),
        check_vma=False,
    )
```

time: 89.2 us -> 71.8 us (0.80)
  Pallas kernels: 87.4 us -> 69.7 us
    pallas_call x1, Pallas kernels: 87.4 us -> 69.7 us  [body(): pl.pallas_call(kernel, out_shape=jax.ShapeDtypeStruct(source.shape, F32),...]
where the time goes in v3:
time: 71.8 us; the launch traced here: 71.4 us
  Pallas kernels  69.7 us (97%)
  local copies, waits for them, and re-layouts  1.67 us (2%)
    pallas_call x1, Pallas kernels, body(): pl.pallas_call(kernel, out_shape=jax.ShapeDtypeStruct(source.shape, F32),...  69.7 us
    unnamed x1, local copies, waits for them, and re-layouts  1.67 us

profile of v3, /device:TPU:448, one launch (start us, length us, event | category | flops | bytes accessed | tf_op | source)
XLA Modules:
  0.0 71.4 jit_solution(287736903758404462)
XLA Ops:
  0.0 69.7 %shard_map.64 = f32[2,256,128]{2,1,0:T(8,128)} custom-call(f32[256,128]{1,0:T(8,128)} %initial.1, f32[2,256,128]{2,1,0:T(8,128)} %source.1, f32[1,128]{1,0:T(1,128)} %bitcast.3, f32[2,2,128,128]{3,2,1,0:T(8,128)} %fine.1, f32[2,2,128,128]{3,2,1,0:T(8,128)} %coarse.1, s32[2,128]{1,0:T(2,128)} %bitcast.2), custom_call_target="tpu_custom_call" | custom-call | tf_op jit(solution)/shard_map/pallas_call | solution.py:601
  69.7 1.7 %copy.8 = f32[2,256,128]{2,1,0:T(8,128)} copy(f32[2,256,128]{2,1,0:T(8,128)} %shard_map.64) | data formatting | bytes 524288

commit v4 on v3

--- a/solution.py
+++ b/solution.py
@@ -36,6 +36,18 @@
 
 def mul(a, weights):
     return halves(jnp.dot(split(a), weights[...], preferred_element_type=F32))
+
+
+def mul_few(a, weights):
+    high = a.astype(BF16)
+    low = (a - high.astype(F32)).astype(BF16)
+    size, width = a.shape
+    both = jnp.dot(
+        jnp.concatenate([high, low], axis=0),
+        weights[0:width, :],
+        preferred_element_type=F32,
+    )
+    return halves(both[:size] + both[size:])
 
 
 def class_sums(onehot, cells):
@@ -83,7 +95,7 @@
 
 def kernel(
     initial, source, mix, fine, coarse, steps, out,
-    wf, wc, wp, wk, state, starts, off, shifted, counts, sums, weights_n, yinit,
+    wf, wc, wp, wk, wl, state, starts, off, shifted, counts, sums, weights_n, yinit,
     fine_p, coarse_p, begun, offy, sbuf, rbuf, many_s, many_r, zs, zr, ys, yr, fin, fin_p,
     kl, kd, ks, kx, kr, ky, kf, kg, kall,
     ssem, rsem, mssem, mrsem, zssem, zrsem, yssem, yrsem, kssem, krsem, pssem, prsem,
@@ -168,6 +180,10 @@
         yinit[g] = padded(class_sums(onehot, initial[rows(g)]))
         for l in range(lead):
             sums[l, g] = padded(class_sums(onehot, source[l, rows(g)]))
+            offy[l, g] = mul_few(sums[l, g], wc.at[l, g])
+        begun[0, g] = yinit[g]
+        begun[1, g] = mul_few(yinit[g], wc.at[0, g]) + offy[0, g]
+        ys[0, g] = mul_few(begun[1, g], wc.at[1, g]) + offy[1, g]
 
     def bulk_setup():
         for g in range(groups):
@@ -256,8 +272,18 @@
         arrived(kall.at[1 - core, batch(b)], k_sems(5, b)[1])
         for l in range(lead):
             for i in range(XS):
-                if b or i < 3:
+                if b or i < 2:
                     put_weights(wk.at[l, b * XS + i], kall[l, b * XS + i])
+            if b == 0:
+                put_weights(wk.at[l, 2], kall[l, 2] + mul(kall[l, 0], wk.at[l, 1]))
+            else:
+                solved = []
+                for d in range(XS):
+                    term = kall[l, XS + d]
+                    for e, earlier in enumerate(solved):
+                        term = term + mul(earlier, wk.at[l, XS + d - 1 - e])
+                    solved.append(term)
+                    wl[l, d] = split(term)
 
     def hop(k, j):
         part = pl.ds(j * chunk, chunk)
@@ -331,21 +357,22 @@
     own_groups, partner_groups = pl.ds(0, groups), pl.ds(groups, groups)
 
     def shared_copies():
-        pairs = [
-            (fine, fine_p),
-            (coarse, coarse_p),
-            (weights_n.at[own_groups], weights_n.at[partner_groups]),
-            (yinit.at[own_groups], yinit.at[partner_groups]),
+        def both(ref):
+            return ref.at[own_groups], ref.at[partner_groups]
+
+        return [
+            both(begun.at[0]), both(begun.at[1]), both(ys.at[0]),
+            both(weights_n), both(yinit), both(sums.at[0]), both(sums.at[1]),
+            both(offy.at[0]), both(offy.at[1]),
+            (coarse, coarse_p), (fine, fine_p),
         ]
-        pairs += [(sums.at[l, own_groups], sums.at[l, partner_groups]) for l in range(lead)]
-        return pairs
 
     @pl.when(jnp.logical_not(lead_core))
     def _():
-        condense()
         pl.semaphore_wait(barrier, len(x_moves) + len(y_moves) + 2)
         for i, (src, dst) in enumerate(shared_copies()):
             send(src, dst, pssem.at[i], prsem.at[i], partner)
+        condense()
         pair_reduce_start(0)
         pair_reduce_start(1)
         bulk_setup()
@@ -373,7 +400,7 @@
         bulk_offsets(1)
         bulk_chain(2)
         bulk_result()
-        arrived(fin_p, prsem.at[7])
+        arrived(fin_p, prsem.at[11])
         result(lambda l, g: fin_p[l, g])
         for i, (src, _) in enumerate(shared_copies()):
             arrived(src, pssem.at[i])
@@ -383,23 +410,24 @@
 
     @pl.when(lead_core)
     def _():
+        bulk_setup()
         condense()
-        bulk_setup()
         pl.semaphore_wait(barrier, len(far_peers) + 2)
         pair_reduce_start(0)
         pair_reduce_start(1)
-        for i, (_, dst) in enumerate(shared_copies()):
-            arrived(dst, prsem.at[i])
-        for g in range(groups):
-            for l in range(lead):
-                put_weights(wf.at[l, groups + g], fine_p[l, g])
-                put_weights(wc.at[l, groups + g], coarse_p[l, g])
-            put_weights(wp.at[groups + g], mul(coarse_p[0, g], wc.at[1, groups + g]))
-
-        @pl.when(tm == 0)
-        def _():
-            for k in range(ITERS + 1):
-                yr[k] = yinit[...]
+        def await_copies(first, end):
+            for i, (_, dst) in enumerate(shared_copies()):
+                if first <= i < end:
+                    arrived(dst, prsem.at[i])
+
+        def prepare():
+            await_copies(3, 10)
+            for g in range(groups):
+                for l in range(lead):
+                    put_weights(wc.at[l, groups + g], coarse_p[l, g])
+                put_weights(wp.at[groups + g], mul(coarse_p[0, g], wc.at[1, groups + g]))
+
+        await_copies(0, 3)
 
         each = [(l, g) for l in range(lead) for g in range(every)]
         used_rows = pl.ds(0, used)
@@ -415,14 +443,14 @@
             )
 
         def row_chain(k):
-            step = [mul(offy[0, g], wc.at[1, g]) + offy[1, g] for g in range(every)]
+            step = [mul_few(offy[0, g], wc.at[1, g]) + offy[1, g] for g in range(every)]
 
             @pl.when(tm > 0)
             def _():
                 row_hop(k).wait_recv()
 
             for g in range(every):
-                ys[k, g] = mul(yr[k, g], wp.at[g]) + step[g]
+                ys[k, g] = mul_few(yr[k, g], wp.at[g]) + step[g]
 
             @pl.when(tm < last)
             def _():
@@ -432,14 +460,14 @@
             y = {}
             for g in range(every):
                 y[0, g] = yr[k, g]
-                y[1, g] = mul(yr[k, g], wc.at[0, g]) + offy[0, g]
+                y[1, g] = mul_few(yr[k, g], wc.at[0, g]) + offy[0, g]
             for l, g in each:
                 begun[l, g] = y[l, g]
             return y
 
         def row_coarse():
             for l, g in each:
-                begun[l, g] = mul(begun[l, g], wc.at[l, g])
+                begun[l, g] = mul_few(begun[l, g], wc.at[l, g])
 
         def row_offsets(y):
             for l, g in each:
@@ -476,12 +504,12 @@
                 fed = old * keep + sums[l, g, 0:size]
                 if average is not None:
                     fed = fed + weights_n[g] * average[l]
-                new = mul(fed, wf.at[l, g])
+                new = mul_few(fed, wf.at[l, g])
                 made[l, g] = jnp.where(limits[0:size] > m, new, old) if m >= FEWEST else new
             return made
 
         def through(row, l, i):
-            return mul(jnp.broadcast_to(row, (8, width)), wk.at[l, i])[0:1]
+            return mul_few(jnp.broadcast_to(row, (8, width)), wk.at[l, i])[0:1]
 
         def late(y, turn, work):
             free = [y]
@@ -492,20 +520,41 @@
             got = exchange_many(turn, own, work)
             fifth = [got[3 * l : 3 * l + 1] for l in range(lead)]
             y = advance(y, 5, fifth)
-            sixth = [got[3 * l + 1 : 3 * l + 2] + through(fifth[l], l, 0) for l in range(lead)]
-            seventh = [got[3 * l + 2 : 3 * l + 3] + through(fifth[l], l, 2) for l in range(lead)]
+            sixth, seventh = [], []
+            for l in range(lead):
+                free_sixth = got[3 * l + 1 : 3 * l + 2]
+                sixth.append(free_sixth + through(fifth[l], l, 0))
+                seventh.append(
+                    got[3 * l + 2 : 3 * l + 3] + through(fifth[l], l, 2) + through(free_sixth, l, 1)
+                )
             y = advance(y, 6, sixth)
-            seventh = [seventh[l] + through(sixth[l], l, 1) for l in range(lead)]
             return advance(y, 7, seventh)
 
-        for l, g in each:
-            offy[l, g] = mul(sums[l, g], wc.at[l, g])
-        row_chain(0)
-        y = row_begin(0)
+        @pl.when(tm == 0)
+        def _():
+            row_hop(0).start()
+
+        @pl.when(tm > 0)
+        def _():
+            prepare()
+            row_chain(0)
+            row_begin(0)
+
+        y = {(l, g): begun[l, g] for l, g in each}
 
         def beside(m):
             def work():
                 if m == 0:
+                    @pl.when(tm == 0)
+                    def _():
+                        prepare()
+                        for k in range(ITERS + 1):
+                            yr[k] = yinit[...]
+
+                    await_copies(10, 11)
+                    for g in range(groups):
+                        for l in range(lead):
+                            put_weights(wf.at[l, groups + g], fine_p[l, g])
                     x_reduce_start(0)
                     row_coarse()
                 elif m == 1:
@@ -556,10 +605,12 @@
 
         got = exchange_many(1, own, work)
         averages = [[got[5 * l + m : 5 * l + m + 1] for m in range(5)] for l in range(lead)]
-        for m in range(4):
-            for l in range(lead):
-                for later in range(m + 1, 5):
-                    averages[l][later] += through(averages[l][m], l, XS + later - m - 1)
+        for l in range(lead):
+            free_rows = jnp.concatenate(averages[l] + [jnp.zeros((3, width), F32)], axis=0)
+            for d in range(1, 5):
+                fed = mul_few(free_rows, wl.at[l, d - 1])
+                for m in range(d, 5):
+                    averages[l][m] = averages[l][m] + fed[m - d : m - d + 1]
         for m in range(5):
             y = advance(y, m, [averages[l][m] for l in range(lead)])
 
@@ -571,10 +622,10 @@
         row_offsets(late(y, 2, work))
         row_chain(2)
         for g in range(every):
-            fin[0, g] = mul(yr[ITERS, g], wc.at[0, g]) + offy[0, g]
+            fin[0, g] = mul_few(yr[ITERS, g], wc.at[0, g]) + offy[0, g]
             fin[1, g] = ys[ITERS, g]
         for l in range(lead):
-            send(fin.at[l, partner_groups], fin_p.at[l], pssem.at[6 + l], prsem.at[7], partner)
+            send(fin.at[l, partner_groups], fin_p.at[l], pssem.at[11 + l], prsem.at[11], partner)
         result(lambda l, g: fin[l, g])
 
         for turn in range(5):
@@ -582,7 +633,7 @@
         for turn, size in ((0, 6), (1, 10), (2, 6)):
             arrived(many_r.at[turn, :, pl.ds(0, size)], mssem.at[turn])
         for l in range(lead):
-            arrived(fin_p.at[l], pssem.at[6 + l])
+            arrived(fin_p.at[l], pssem.at[11 + l])
         drain_common()
 
         @pl.when(tm < last)
@@ -608,6 +659,7 @@
             pltpu.VMEM((lead, every, 2 * width, 2 * width), BF16),
             pltpu.VMEM((every, 2 * width, 2 * width), BF16),
             pltpu.VMEM((lead, mats, 2 * width, 2 * width), BF16),
+            pltpu.VMEM((lead, XS, width, 2 * width), BF16),
             pltpu.VMEM((lead, count, width), F32),
             pltpu.VMEM((lead, count, width), F32),
             pltpu.VMEM((lead, count, width), F32),
@@ -649,8 +701,8 @@
             pltpu.SemaphoreType.DMA((ITERS + 1,)),
             pltpu.SemaphoreType.DMA((12,)),
             pltpu.SemaphoreType.DMA((12,)),
-            pltpu.SemaphoreType.DMA((8,)),
-            pltpu.SemaphoreType.DMA((8,)),
+            pltpu.SemaphoreType.DMA((13,)),
+            pltpu.SemaphoreType.DMA((13,)),
         ],
         compiler_params=pltpu.CompilerParams(collective_id=0, has_side_effects=True),
     )(

time: 71.8 us -> 69.7 us (0.971)
  Pallas kernels: 69.7 us -> 67.6 us
    pallas_call x1, Pallas kernels: 69.7 us -> 67.6 us  [body(): pl.pallas_call(kernel, out_shape=jax.ShapeDtypeStruct(source.shape, F32),...]
where the time goes in v4:
time: 69.7 us; the launch traced here: 69.3 us
  Pallas kernels  67.6 us (97%)
  local copies, waits for them, and re-layouts  1.67 us (2%)
    pallas_call x1, Pallas kernels, body(): pl.pallas_call(kernel, out_shape=jax.ShapeDtypeStruct(source.shape, F32),...  67.6 us
    unnamed x1, local copies, waits for them, and re-layouts  1.67 us

profile of v4, /device:TPU:448, one launch (start us, length us, event | category | flops | bytes accessed | tf_op | source)
XLA Modules:
  0.0 69.3 jit_solution(14856645687707391239)
XLA Ops:
  0.0 67.6 %shard_map.64 = f32[2,256,128]{2,1,0:T(8,128)} custom-call(f32[256,128]{1,0:T(8,128)} %initial.1, f32[2,256,128]{2,1,0:T(8,128)} %source.1, f32[1,128]{1,0:T(1,128)} %bitcast.3, f32[2,2,128,128]{3,2,1,0:T(8,128)} %fine.1, f32[2,2,128,128]{3,2,1,0:T(8,128)} %coarse.1, s32[2,128]{1,0:T(2,128)} %bitcast.2), custom_call_target="tpu_custom_call" | custom-call | tf_op jit(solution)/shard_map/pallas_call | solution.py:652
  67.6 1.7 %copy.8 = f32[2,256,128]{2,1,0:T(8,128)} copy(f32[2,256,128]{2,1,0:T(8,128)} %shard_map.64) | data formatting | bytes 524288

commit v5 on v4

--- a/solution.py
+++ b/solution.py
@@ -571,13 +571,16 @@
                     y_reduce_start(1)
                     for i in range(4, FINE_MAX):
                         fine_cells(i)
+                    bulk_offsets(0)
                 elif m == 4:
                     y_gather_start(1)
                     x_gather_done(0)
-                    bulk_offsets(0)
+                    bulk_chain(1)
                 else:
                     x_gather_start(1)
-                    bulk_chain(1)
+                    bulk_begin(1)
+                    for i in range(4):
+                        fine_cells(i)
                     k_finish(0)
 
             return work
@@ -597,8 +600,7 @@
 
         def work():
             row_coarse()
-            bulk_begin(1)
-            for m in range(FINE_MAX):
+            for m in range(4, FINE_MAX):
                 fine_cells(m)
             x_gather_done(1)
             k_finish(1)
@@ -621,11 +623,15 @@
 
         row_offsets(late(y, 2, work))
         row_chain(2)
-        for g in range(every):
-            fin[0, g] = mul_few(yr[ITERS, g], wc.at[0, g]) + offy[0, g]
-            fin[1, g] = ys[ITERS, g]
+        def ends(these):
+            for g in these:
+                fin[0, g] = mul_few(yr[ITERS, g], wc.at[0, g]) + offy[0, g]
+                fin[1, g] = ys[ITERS, g]
+
+        ends(range(groups, every))
         for l in range(lead):
             send(fin.at[l, partner_groups], fin_p.at[l], pssem.at[11 + l], prsem.at[11], partner)
+        ends(range(groups))
         result(lambda l, g: fin[l, g])
 
         for turn in range(5):

time: 69.7 us -> 69.6 us (level)
  no operation moved by 1% of the time
where the time goes in v5:
time: 69.6 us; the launch traced here: 69.3 us
  Pallas kernels  67.6 us (97%)
  local copies, waits for them, and re-layouts  1.67 us (2%)
    pallas_call x1, Pallas kernels, body(): pl.pallas_call(kernel, out_shape=jax.ShapeDtypeStruct(source.shape, F32),...  67.6 us
    unnamed x1, local copies, waits for them, and re-layouts  1.67 us

profile of v5, /device:TPU:448, one launch (start us, length us, event | category | flops | bytes accessed | tf_op | source)
XLA Modules:
  0.0 69.3 jit_solution(9508475298345135294)
XLA Ops:
  0.0 67.6 %shard_map.64 = f32[2,256,128]{2,1,0:T(8,128)} custom-call(f32[256,128]{1,0:T(8,128)} %initial.1, f32[2,256,128]{2,1,0:T(8,128)} %source.1, f32[1,128]{1,0:T(1,128)} %bitcast.3, f32[2,2,128,128]{3,2,1,0:T(8,128)} %fine.1, f32[2,2,128,128]{3,2,1,0:T(8,128)} %coarse.1, s32[2,128]{1,0:T(2,128)} %bitcast.2), custom_call_target="tpu_custom_call" | custom-call | tf_op jit(solution)/shard_map/pallas_call | solution.py:658
  67.6 1.7 %copy.8 = f32[2,256,128]{2,1,0:T(8,128)} copy(f32[2,256,128]{2,1,0:T(8,128)} %shard_map.64) | data formatting | bytes 524288
